TPU v7x, 32 devices: a whole 2x2x4 slice. The times are simulated.
32 devices in a mesh: lon: 8 (over y, x, core), lat: 4 (over z).
Axes of the slice: x: 2, y: 2, z: 4, core: 2. Of those that a mesh axis runs over, the one named last changes fastest.
Arguments:
- surface_forcing: float32 [96, 1024], P('lat', 'lon'), may hold values from -33 to 33
- sea_mask: int32 [96, 1024], P('lat', 'lon'), may hold values 0 or 1
- level_count: int32 [96, 1024], P('lat', 'lon'), may hold values from 1 to 40
- state: float32 [4, 40, 96, 1024], P(None, None, 'lat', 'lon'), may hold values from -6 to 6
Outputs:
- surface_height: float32 [96, 1024], P('lat', 'lon')
- residual: float32 [96, 1024], P('lat', 'lon')
- tendency: float32 [4, 40, 96, 1024], P(None, None, 'lat', 'lon')
All inputs are finite; a program needn't handle non-finite values. No bound on the sum of `sea_mask` on one device may be relied on, other than what follows from the above.
Results may differ from a plain program's by a relative error of at most 0.0003.
Values sent between devices are 32-bit elements; how exact they have to be, the bound alone decides.
No kernel may reach another device: no remote copies, remote signals or barrier semaphores. Data moves between devices by JAX's collectives and lax.ppermute only.
A program may use at most 64 MiB of HBM per device.

v0:
```python
import jax
import jax.numpy as jnp
from jax import lax
from jax.sharding import PartitionSpec as P

LEV = 40
ITERS = 4


damping = 0.05
face_scale = 1.0
viscosity = 0.02


def with_halo(cells, sides, width):
    for axis, dim in sides:
        count = lax.axis_size(axis)
        head = lax.slice_in_dim(cells, 0, width, axis=dim)
        tail = lax.slice_in_dim(cells, cells.shape[dim] - width, cells.shape[dim], axis=dim)
        cells = jnp.concatenate(
            [
                lax.ppermute(tail, axis, [(i, (i + 1) % count) for i in range(count)]),
                cells,
                lax.ppermute(head, axis, [((i + 1) % count, i) for i in range(count)]),
            ],
            axis=dim,
        )
    return cells


def trim_rims(field, margin):
    return field[..., margin : field.shape[-2] - margin, margin : field.shape[-1] - margin]


def face_coeffs(depth, width_out, width_in):
    offset = width_in - width_out
    height = depth.shape[0] - 2 * offset
    breadth = depth.shape[1] - 2 * offset
    center = depth[offset : offset + height, offset : offset + breadth]
    east_face = face_scale * jnp.minimum(
        center, depth[offset : offset + height, offset + 1 : offset + 1 + breadth]
    )
    west_face = face_scale * jnp.minimum(
        center, depth[offset : offset + height, offset - 1 : offset - 1 + breadth]
    )
    north_face = face_scale * jnp.minimum(
        center, depth[offset + 1 : offset + 1 + height, offset : offset + breadth]
    )
    south_face = face_scale * jnp.minimum(
        center, depth[offset - 1 : offset - 1 + height, offset : offset + breadth]
    )
    diagonal = damping + east_face + west_face + north_face + south_face
    return (diagonal, east_face, west_face, north_face, south_face)


def operator_apply(padded, coeffs):
    diagonal, east_face, west_face, north_face, south_face = coeffs
    return (
        diagonal * padded[1:-1, 1:-1]
        - east_face * padded[1:-1, 2:]
        - west_face * padded[1:-1, :-2]
        - north_face * padded[2:, 1:-1]
        - south_face * padded[:-2, 1:-1]
    )


def laplace(field, active):
    center = field[..., 1:-1, 1:-1]
    active_center = active[..., 1:-1, 1:-1]
    east_part = active_center * active[..., 1:-1, 2:] * (field[..., 1:-1, 2:] - center)
    west_part = active_center * active[..., 1:-1, :-2] * (center - field[..., 1:-1, :-2])
    north_part = active_center * active[..., 2:, 1:-1] * (field[..., 2:, 1:-1] - center)
    south_part = active_center * active[..., :-2, 1:-1] * (center - field[..., :-2, 1:-1])
    return east_part - west_part + north_part - south_part


def advect(field, active):
    east_flow = field[2]
    north_flow = field[3]
    center = field[..., 1:-1, 1:-1]
    active_center = active[..., 1:-1, 1:-1]
    flow_center = east_flow[..., 1:-1, 1:-1]
    lift_center = north_flow[..., 1:-1, 1:-1]
    east_speed = (
        0.25 * active_center * active[..., 1:-1, 2:] * (flow_center + east_flow[..., 1:-1, 2:])
    )
    west_speed = (
        0.25 * active_center * active[..., 1:-1, :-2] * (flow_center + east_flow[..., 1:-1, :-2])
    )
    north_speed = (
        0.25 * active_center * active[..., 2:, 1:-1] * (lift_center + north_flow[..., 2:, 1:-1])
    )
    south_speed = (
        0.25 * active_center * active[..., :-2, 1:-1] * (lift_center + north_flow[..., :-2, 1:-1])
    )
    return (
        east_speed * (center + field[..., 1:-1, 2:])
        - west_speed * (center + field[..., 1:-1, :-2])
        + north_speed * (center + field[..., 2:, 1:-1])
        - south_speed * (center + field[..., :-2, 1:-1])
    )


def tendency_of(state_wide, active_wide):
    inner_active = trim_rims(active_wide, 1)
    smoothed = laplace(laplace(state_wide, active_wide), inner_active)
    flux = advect(trim_rims(state_wide, 1), inner_active)
    return trim_rims(active_wide, 2) * (-flux - viscosity * smoothed)


def apply_operator(field, coeff_list):
    padded = with_halo(field, (("lon", 1), ("lat", 0)), 1)
    return (operator_apply(padded, coeff_list[0]), 0)


def paired_totals(residual, search, image, width):
    return lax.psum(
        (jnp.sum(trim_rims(residual * search, width)), jnp.sum(trim_rims(image * search, width))),
        ("lon", "lat"),
    )


def paired_solve(forcing, width, coeff_list):
    residual = forcing
    search = residual / coeff_list[width][0]
    image, narrow = apply_operator(search, coeff_list)
    residual = trim_rims(residual, width - narrow)
    search = trim_rims(search, width - narrow)
    width = narrow
    product, curvature = paired_totals(residual, search, image, width)
    alpha_step = product / curvature
    direction = search
    along = image
    solution = jnp.zeros_like(residual)
    for step_index in range(ITERS):
        solution = solution + alpha_step * direction
        residual = residual - alpha_step * along
        if step_index + 1 < ITERS:
            search = residual / coeff_list[width][0]
            image, narrow = apply_operator(search, coeff_list)
            margin = width - narrow
            residual = trim_rims(residual, margin)
            search = trim_rims(search, margin)
            solution = trim_rims(solution, margin)
            direction = trim_rims(direction, margin)
            along = trim_rims(along, margin)
            width = narrow
            product_next, curvature = paired_totals(residual, search, image, width)
            beta_step = product_next / product
            alpha_step = product_next / (curvature - beta_step * product_next / alpha_step)
            product = product_next
            direction = search + beta_step * direction
            along = image + beta_step * along
    return (solution, residual)


def per_device(surface_forcing, sea_mask, level_count, state):
    height = surface_forcing.shape[0]
    rim_width = 2
    columns = jnp.stack([sea_mask, level_count])
    columns_wide = with_halo(columns, (("lon", 2), ("lat", 1)), rim_width)
    rows_global = (
        lax.axis_index("lat") * height
        + jnp.arange(height + 2 * rim_width, dtype=jnp.int32)
        - rim_width
    )
    inside = ((rows_global >= 0) & (rows_global < height * lax.axis_size("lat"))).astype(
        jnp.float32
    )
    sea_wide = columns_wide[0].astype(jnp.float32) * inside[:, None]
    depth = sea_wide * columns_wide[1].astype(jnp.float32) / LEV
    coeff_list = [face_coeffs(depth, width, rim_width) for width in range(rim_width)]
    forcing = trim_rims(sea_wide, rim_width) * surface_forcing
    start_width = 0
    solution, residual = paired_solve(forcing, start_width, coeff_list)
    level_index = jnp.arange(state.shape[1], dtype=jnp.int32)[:, None, None]
    sea_near = trim_rims(sea_wide, rim_width - 2)
    count_near = trim_rims(columns_wide[1], rim_width - 2)
    active_wide = (level_index < count_near[None]).astype(jnp.float32) * sea_near[None]
    state_wide = with_halo(state, (("lon", 3), ("lat", 2)), 2)
    tendency = tendency_of(state_wide, active_wide)
    return (solution, residual, tendency)


def solution(mesh):
    return jax.shard_map(
        per_device,
        mesh=mesh,
        in_specs=(P("lat", "lon"), P("lat", "lon"), P("lat", "lon"), P(None, None, "lat", "lon")),
        out_specs=(P("lat", "lon"), P("lat", "lon"), P(None, None, "lat", "lon")),
        check_vma=False,
    )
```

profile of v0, /device:TPU:0, one launch (start us, length us, event | category | flops | bytes accessed | tf_op | source)
XLA Modules:
  0.0 297.8 jit_solution(5323145204198029798)
XLA Ops:
  2.0 2.9 collective-permute-start.1
  4.9 4.1 %fusion.74 = (f32[4,40,24,2]{3,2,1,0:T(8,128)S(1)}, f32[4,40,24,2]{3,2,1,0:T(8,128)}) fusion(f32[4,40,24,128]{3,2,1,0:T(8,128)} %param.7), kind=kLoop, calls=%fused_computation.183 | loop fusion | bytes 122880 | tf_op jit(solution)/shard_map/slice | solution.py:19
  9.0 2.3 copy.22
  13.5 2.2 collective-permute-start.2
  15.7 2.1 collective-permute-start.3
  17.8 1.9 copy.10
  20.1 2.6 collective-permute-start.4
  24.2 3.5 %collective-permute-start.6 = (f32[1,130]{1,0:T(1,128)S(1)}, f32[1,130]{1,0:T(1,128)S(1)}, u32[]{:S(2)}, u32[]{:S(2)}) collective-permute-start(f32[1,130]{1,0:T(1,128)S(1)} %get-tuple-element.69), channel_id=1, source_target_pairs={{1,0},{2,1},{3,2},{0,3},{5,4},{6,5},{7,6},{4,7},{9,8},{10,9},{11,1... | collective-permute-start | bytes 1568 | tf_op jit(solution)/shard_map/ppermute | solution.py:24
  28.9 4.1 %collective-permute-done.7 = f32[1,130]{1,0:T(1,128)S(1)} collective-permute-done((f32[1,130]{1,0:T(1,128)S(1)}, f32[1,130]{1,0:T(1,128)S(1)}, u32[]{:S(2)}, u32[]{:S(2)}) %collective-permute-start.7) | collective-permute-done | bytes 552 | tf_op jit(solution)/shard_map/ppermute | solution.py:22
  33.7 37.2 %all-reduce.3 = (f32[]{:T(128)}, f32[]{:T(128)}) all-reduce(f32[]{:T(128)} %get-tuple-element.13, f32[]{:T(128)} %get-tuple-element.12), channel_id=1, replica_groups=mesh['lon'=8,'lat'=4] {'lon','lat'}, use_global_device_ids=true, to_apply=%region_1.0 | all-reduce | flops 2 | bytes 16 | tf_op jit(solution)/shard_map/psum | solution.py:117
  72.4 2.6 collective-permute-start.8
  76.5 2.3 collective-permute-start.10
  80.8 3.3 %collective-permute-done.11 = f32[1,130]{1,0:T(1,128)S(1)} collective-permute-done((f32[1,130]{1,0:T(1,128)S(1)}, f32[1,130]{1,0:T(1,128)S(1)}, u32[]{:S(2)}, u32[]{:S(2)}) %collective-permute-start.11) | collective-permute-done | bytes 552 | tf_op jit(solution)/shard_map/ppermute | solution.py:22
  84.9 38.5 %all-reduce.2 = (f32[]{:T(128)}, f32[]{:T(128)}) all-reduce(f32[]{:T(128)} %get-tuple-element.11, f32[]{:T(128)} %get-tuple-element.10), channel_id=1, replica_groups=mesh['lon'=8,'lat'=4] {'lon','lat'}, use_global_device_ids=true, to_apply=%region_5.0 | all-reduce | flops 2 | bytes 16 | tf_op jit(solution)/shard_map/psum | solution.py:117
  128.0 2.6 collective-permute-start.12
  132.1 2.3 collective-permute-start.14
  136.3 3.5 %collective-permute-done.15 = f32[1,130]{1,0:T(1,128)S(1)} collective-permute-done((f32[1,130]{1,0:T(1,128)S(1)}, f32[1,130]{1,0:T(1,128)S(1)}, u32[]{:S(2)}, u32[]{:S(2)}) %collective-permute-start.15) | collective-permute-done | bytes 552 | tf_op jit(solution)/shard_map/ppermute | solution.py:22
  140.5 38.1 %all-reduce.1 = (f32[]{:T(128)}, f32[]{:T(128)}) all-reduce(f32[]{:T(128)} %get-tuple-element.9, f32[]{:T(128)} %get-tuple-element.8), channel_id=1, replica_groups=mesh['lon'=8,'lat'=4] {'lon','lat'}, use_global_device_ids=true, to_apply=%region_9.0 | all-reduce | flops 2 | bytes 16 | tf_op jit(solution)/shard_map/psum | solution.py:117
  182.3 2.6 collective-permute-start.16
  186.4 2.3 collective-permute-start.18
  189.2 3.2 %slice_multiply_fusion.3 = (f32[40,26,130]{2,0,1:T(8,128)}, f32[40,26,130]{2,0,1:T(8,128)}, f32[40,26,130]{2,0,1:T(8,128)}, f32[40,26,130]{2,0,1:T(8,128)}) fusion(f32[40,28,132]{2,0,1:T(8,128)S(1)} %fusion.29), kind=kLoop, calls=%fused_computation.51 | loop fusion | flops 540800 | bytes 4867200 | tf_op jit(solution)/shard_map/mul | solution.py:70
  192.4 1.7 collective-permute-done.19
  195.4 39.5 %all-reduce = (f32[]{:T(128)}, f32[]{:T(128)}) all-reduce(f32[]{:T(128)} %get-tuple-element.7, f32[]{:T(128)} %get-tuple-element.6), channel_id=1, replica_groups=mesh['lon'=8,'lat'=4] {'lon','lat'}, use_global_device_ids=true, to_apply=%region_13.0 | all-reduce | flops 2 | bytes 16 | tf_op jit(solution)/shard_map/psum | solution.py:117
  238.7 2.9 copy.9
  241.6 2.0 copy.11
  247.9 7.0 %collective-permute-done.23 = f32[4,40,2,132]{3,1,2,0:T(8,128)S(1)} collective-permute-done((f32[4,40,2,132]{3,1,2,0:T(8,128)S(1)}, f32[4,40,2,132]{3,1,2,0:T(8,128)S(1)}, u32[]{:S(2)}, u32[]{:S(2)}) %collective-permute-start.23) | collective-permute-done | bytes 168992 | tf_op jit(solution)/shard_map/ppermute | solution.py:24
  255.0 7.6 %collective-permute-done.22 = f32[4,40,2,132]{3,1,2,0:T(8,128)S(1)} collective-permute-done((f32[4,40,2,132]{3,1,2,0:T(8,128)S(1)}, f32[4,40,2,132]{3,1,2,0:T(8,128)S(1)}, u32[]{:S(2)}, u32[]{:S(2)}) %collective-permute-start.22) | collective-permute-done | bytes 168992 | tf_op jit(solution)/shard_map/ppermute | solution.py:22
  263.3 2.1 pad_maximum_fusion
  267.6 2.9 fusion.75
  270.6 11.5 %fusion.2 = f32[4,40,26,130]{3,1,2,0:T(8,128)} fusion(f32[4,40,2,132]{3,1,2,0:T(8,128)} %copy-done.7, f32[4,40,24,2]{3,1,2,0:T(8,128)S(1)} %copy-done.1, f32[4,40,24,128]{3,1,2,0:T(8,128)S(1)} %copy.10, f32[4,40,24,2]{3,1,2,0:T(8,128)S(1)} %copy-done, f32[4,40,2,132]{3,1,2,0:T(8,128)} %copy-done.5, f32[4,40,28,132]{3,1,2,0:T(8,128)S(1)} %pad_maximum_fusion, ...), kind=kLoop, calls=%fused_computation.4 | loop fusion | flops 9193600 | bytes 13181440 | tf_op jit(solution)/shard_map/sub | solution.py:74
  282.1 12.6 %fusion.13 = f32[4,40,24,128]{3,1,2,0:T(8,128)} fusion(f32[4,40,26,130]{3,1,2,0:T(8,128)} %fusion.2, f32[4,40,24,128]{3,1,2,0:T(8,128)S(1)} %copy.10, f32[4,40,2,132]{3,1,2,0:T(8,128)S(1)} %copy-done.8, f32[4,40,24,2]{3,1,2,0:T(8,128)} %copy.11, f32[4,40,24,2]{3,1,2,0:T(8,128)S(1)} %copy-done, f32[4,40,2,132]{3,1,2,0:T(8,128)S(1)} %copy-done.6, ...), kind=kLoop, calls=%fused_computation.23 | loop fusion | flops 16711680 | bytes 18585600 | tf_op jit(solution)/shard_map/mul | solution.py:108
  294.7 3.2 %copy.20 = f32[4,40,24,128]{3,2,1,0:T(8,128)} copy(f32[4,40,24,128]{3,1,2,0:T(8,128)} %fusion.13) | data formatting | bytes 3932160
  (92 shorter events, 26.7 us)
Async XLA Ops:
  1.5 11.9 %collective-permute-start = (s32[2,24,2]{2,1,0:T(8,128)S(1)}, s32[2,24,2]{2,1,0:T(8,128)S(1)}, u32[]{:S(2)}, u32[]{:S(2)}) collective-permute-start(s32[2,24,2]{2,1,0:T(8,128)S(1)} %get-tuple-element.71), channel_id=1, source_target_pairs={{0,4},{4,8},{8,12},{12,16},{16,20},{20,24},{24,28},{28,0},{1,5},{5... | collective-permute-start | bytes 1160 | tf_op jit(solution)/shard_map/ppermute | solution.py:22
  2.0 11.4 %collective-permute-start.1 = (s32[2,24,2]{2,1,0:T(8,128)S(1)}, s32[2,24,2]{2,1,0:T(8,128)S(1)}, u32[]{:S(2)}, u32[]{:S(2)}) collective-permute-start(s32[2,24,2]{2,1,0:T(8,128)S(1)} %get-tuple-element.72), channel_id=1, source_target_pairs={{4,0},{8,4},{12,8},{16,12},{20,16},{24,20},{28,24},{0,28},{5,1},{9... | collective-permute-start | bytes 1160 | tf_op jit(solution)/shard_map/ppermute | solution.py:24
  9.0 4.4 %copy-start.11 = (s32[24,128]{1,0:T(8,128)S(1)}, s32[24,128]{1,0:T(8,128)}, u32[]{:S(2)}) copy-start(s32[24,128]{1,0:T(8,128)} %param.5) | copy-start | bytes 36868
  11.3 230.3 %collective-permute-start.21 = (f32[4,40,24,2]{1,2,3,0:T(8,128)S(1)}, f32[4,40,24,2]{1,2,3,0:T(8,128)S(1)}, u32[]{:S(2)}, u32[]{:S(2)}) collective-permute-start(f32[4,40,24,2]{1,2,3,0:T(8,128)S(1)} %copy.22), channel_id=1, source_target_pairs={{4,0},{8,4},{12,8},{16,12},{20,16},{24,20},{28,24},{0,28},{5,1},{9... | collective-permute-start | bytes 92168 | tf_op jit(solution)/shard_map/ppermute | solution.py:24
  13.4 225.3 %collective-permute-start.20 = (f32[4,40,24,2]{1,2,3,0:T(8,128)}, f32[4,40,24,2]{1,2,3,0:T(8,128)}, u32[]{:S(2)}, u32[]{:S(2)}) collective-permute-start(f32[4,40,24,2]{1,2,3,0:T(8,128)} %copy.21), channel_id=1, source_target_pairs={{0,4},{4,8},{8,12},{12,16},{16,20},{20,24},{24,28},{28,0},{1,5},{5... | collective-permute-start | bytes 92168 | tf_op jit(solution)/shard_map/ppermute | solution.py:22
  13.5 6.2 %collective-permute-start.2 = (s32[2,2,132]{2,1,0:T(2,128)S(1)}, s32[2,2,132]{2,1,0:T(2,128)S(1)}, u32[]{:S(2)}, u32[]{:S(2)}) collective-permute-start(s32[2,2,132]{2,1,0:T(2,128)S(1)} %get-tuple-element.61), channel_id=1, source_target_pairs={{0,1},{1,2},{2,3},{3,0},{4,5},{5,6},{6,7},{7,4},{8,9},{9,10},{10,1... | collective-permute-start | bytes 6344 | tf_op jit(solution)/shard_map/ppermute | solution.py:22
  15.7 4.0 %collective-permute-start.3 = (s32[2,2,132]{2,1,0:T(2,128)S(1)}, s32[2,2,132]{2,1,0:T(2,128)S(1)}, u32[]{:S(2)}, u32[]{:S(2)}) collective-permute-start(s32[2,2,132]{2,1,0:T(2,128)S(1)} %get-tuple-element.62), channel_id=1, source_target_pairs={{1,0},{2,1},{3,2},{0,3},{5,4},{6,5},{7,6},{4,7},{9,8},{10,9},{11,1... | collective-permute-start | bytes 6344 | tf_op jit(solution)/shard_map/ppermute | solution.py:24
  20.0 4.0 %collective-permute-start.5 = (f32[24,1]{1,0:T(8,128)S(1)}, f32[24,1]{1,0:T(8,128)S(1)}, u32[]{:S(2)}, u32[]{:S(2)}) collective-permute-start(f32[24,1]{1,0:T(8,128)S(1)} %get-tuple-element.79), channel_id=1, source_target_pairs={{0,4},{4,8},{8,12},{12,16},{16,20},{20,24},{24,28},{28,0},{1,5},{5... | collective-permute-start | bytes 296 | tf_op jit(solution)/shard_map/ppermute | solution.py:22
  20.1 4.0 %collective-permute-start.4 = (f32[24,1]{1,0:T(8,128)S(1)}, f32[24,1]{1,0:T(8,128)S(1)}, u32[]{:S(2)}, u32[]{:S(2)}) collective-permute-start(f32[24,1]{1,0:T(8,128)S(1)} %get-tuple-element.80), channel_id=1, source_target_pairs={{4,0},{8,4},{12,8},{16,12},{20,16},{24,20},{28,24},{0,28},{5,1},{9... | collective-permute-start | bytes 296 | tf_op jit(solution)/shard_map/ppermute | solution.py:24
  24.2 4.8 %collective-permute-start.6 = (f32[1,130]{1,0:T(1,128)S(1)}, f32[1,130]{1,0:T(1,128)S(1)}, u32[]{:S(2)}, u32[]{:S(2)}) collective-permute-start(f32[1,130]{1,0:T(1,128)S(1)} %get-tuple-element.69), channel_id=1, source_target_pairs={{1,0},{2,1},{3,2},{0,3},{5,4},{6,5},{7,6},{4,7},{9,8},{10,9},{11,1... | collective-permute-start | bytes 1568 | tf_op jit(solution)/shard_map/ppermute | solution.py:24
  27.6 5.4 %collective-permute-start.7 = (f32[1,130]{1,0:T(1,128)S(1)}, f32[1,130]{1,0:T(1,128)S(1)}, u32[]{:S(2)}, u32[]{:S(2)}) collective-permute-start(f32[1,130]{1,0:T(1,128)S(1)} %get-tuple-element.70), channel_id=1, source_target_pairs={{0,1},{1,2},{2,3},{3,0},{4,5},{5,6},{6,7},{7,4},{8,9},{9,10},{10,1... | collective-permute-start | bytes 1568 | tf_op jit(solution)/shard_map/ppermute | solution.py:22
  72.4 4.0 %collective-permute-start.9 = (f32[24,1]{1,0:T(8,128)S(1)}, f32[24,1]{1,0:T(8,128)S(1)}, u32[]{:S(2)}, u32[]{:S(2)}) collective-permute-start(f32[24,1]{1,0:T(8,128)S(1)} %get-tuple-element.77), channel_id=1, source_target_pairs={{0,4},{4,8},{8,12},{12,16},{16,20},{20,24},{24,28},{28,0},{1,5},{5... | collective-permute-start | bytes 296 | tf_op jit(solution)/shard_map/ppermute | solution.py:22
  72.4 4.1 %collective-permute-start.8 = (f32[24,1]{1,0:T(8,128)S(1)}, f32[24,1]{1,0:T(8,128)S(1)}, u32[]{:S(2)}, u32[]{:S(2)}) collective-permute-start(f32[24,1]{1,0:T(8,128)S(1)} %get-tuple-element.78), channel_id=1, source_target_pairs={{4,0},{8,4},{12,8},{16,12},{20,16},{24,20},{28,24},{0,28},{5,1},{9... | collective-permute-start | bytes 296 | tf_op jit(solution)/shard_map/ppermute | solution.py:24
  76.5 4.3 %collective-permute-start.10 = (f32[1,130]{1,0:T(1,128)S(1)}, f32[1,130]{1,0:T(1,128)S(1)}, u32[]{:S(2)}, u32[]{:S(2)}) collective-permute-start(f32[1,130]{1,0:T(1,128)S(1)} %get-tuple-element.67), channel_id=1, source_target_pairs={{1,0},{2,1},{3,2},{0,3},{5,4},{6,5},{7,6},{4,7},{9,8},{10,9},{11,1... | collective-permute-start | bytes 1568 | tf_op jit(solution)/shard_map/ppermute | solution.py:24
  78.8 5.4 %collective-permute-start.11 = (f32[1,130]{1,0:T(1,128)S(1)}, f32[1,130]{1,0:T(1,128)S(1)}, u32[]{:S(2)}, u32[]{:S(2)}) collective-permute-start(f32[1,130]{1,0:T(1,128)S(1)} %get-tuple-element.68), channel_id=1, source_target_pairs={{0,1},{1,2},{2,3},{3,0},{4,5},{5,6},{6,7},{7,4},{8,9},{9,10},{10,1... | collective-permute-start | bytes 1568 | tf_op jit(solution)/shard_map/ppermute | solution.py:22
  128.0 4.0 %collective-permute-start.13 = (f32[24,1]{1,0:T(8,128)S(1)}, f32[24,1]{1,0:T(8,128)S(1)}, u32[]{:S(2)}, u32[]{:S(2)}) collective-permute-start(f32[24,1]{1,0:T(8,128)S(1)} %get-tuple-element.75), channel_id=1, source_target_pairs={{0,4},{4,8},{8,12},{12,16},{16,20},{20,24},{24,28},{28,0},{1,5},{5... | collective-permute-start | bytes 296 | tf_op jit(solution)/shard_map/ppermute | solution.py:22
  128.0 4.0 %collective-permute-start.12 = (f32[24,1]{1,0:T(8,128)S(1)}, f32[24,1]{1,0:T(8,128)S(1)}, u32[]{:S(2)}, u32[]{:S(2)}) collective-permute-start(f32[24,1]{1,0:T(8,128)S(1)} %get-tuple-element.76), channel_id=1, source_target_pairs={{4,0},{8,4},{12,8},{16,12},{20,16},{24,20},{28,24},{0,28},{5,1},{9... | collective-permute-start | bytes 296 | tf_op jit(solution)/shard_map/ppermute | solution.py:24
  132.1 4.1 %collective-permute-start.14 = (f32[1,130]{1,0:T(1,128)S(1)}, f32[1,130]{1,0:T(1,128)S(1)}, u32[]{:S(2)}, u32[]{:S(2)}) collective-permute-start(f32[1,130]{1,0:T(1,128)S(1)} %get-tuple-element.65), channel_id=1, source_target_pairs={{1,0},{2,1},{3,2},{0,3},{5,4},{6,5},{7,6},{4,7},{9,8},{10,9},{11,1... | collective-permute-start | bytes 1568 | tf_op jit(solution)/shard_map/ppermute | solution.py:24
  134.4 5.4 %collective-permute-start.15 = (f32[1,130]{1,0:T(1,128)S(1)}, f32[1,130]{1,0:T(1,128)S(1)}, u32[]{:S(2)}, u32[]{:S(2)}) collective-permute-start(f32[1,130]{1,0:T(1,128)S(1)} %get-tuple-element.66), channel_id=1, source_target_pairs={{0,1},{1,2},{2,3},{3,0},{4,5},{5,6},{6,7},{7,4},{8,9},{9,10},{10,1... | collective-permute-start | bytes 1568 | tf_op jit(solution)/shard_map/ppermute | solution.py:22
  182.2 11.9 %copy-start.13 = (f32[24,128]{1,0:T(8,128)}, f32[24,128]{1,0:T(8,128)S(1)}, u32[]{:S(2)}) copy-start(f32[24,128]{1,0:T(8,128)S(1)} %get-tuple-element.24) | copy-start | bytes 36868
  182.3 4.0 %collective-permute-start.17 = (f32[24,1]{1,0:T(8,128)S(1)}, f32[24,1]{1,0:T(8,128)S(1)}, u32[]{:S(2)}, u32[]{:S(2)}) collective-permute-start(f32[24,1]{1,0:T(8,128)S(1)} %get-tuple-element.73), channel_id=1, source_target_pairs={{0,4},{4,8},{8,12},{12,16},{16,20},{20,24},{24,28},{28,0},{1,5},{5... | collective-permute-start | bytes 296 | tf_op jit(solution)/shard_map/ppermute | solution.py:22
  182.3 4.0 %collective-permute-start.16 = (f32[24,1]{1,0:T(8,128)S(1)}, f32[24,1]{1,0:T(8,128)S(1)}, u32[]{:S(2)}, u32[]{:S(2)}) collective-permute-start(f32[24,1]{1,0:T(8,128)S(1)} %get-tuple-element.74), channel_id=1, source_target_pairs={{4,0},{8,4},{12,8},{16,12},{20,16},{24,20},{28,24},{0,28},{5,1},{9... | collective-permute-start | bytes 296 | tf_op jit(solution)/shard_map/ppermute | solution.py:24
  186.4 5.9 %collective-permute-start.18 = (f32[1,130]{1,0:T(1,128)S(1)}, f32[1,130]{1,0:T(1,128)S(1)}, u32[]{:S(2)}, u32[]{:S(2)}) collective-permute-start(f32[1,130]{1,0:T(1,128)S(1)} %get-tuple-element.63), channel_id=1, source_target_pairs={{1,0},{2,1},{3,2},{0,3},{5,4},{6,5},{7,6},{4,7},{9,8},{10,9},{11,1... | collective-permute-start | bytes 1568 | tf_op jit(solution)/shard_map/ppermute | solution.py:24
  188.7 5.4 %collective-permute-start.19 = (f32[1,130]{1,0:T(1,128)S(1)}, f32[1,130]{1,0:T(1,128)S(1)}, u32[]{:S(2)}, u32[]{:S(2)}) collective-permute-start(f32[1,130]{1,0:T(1,128)S(1)} %get-tuple-element.64), channel_id=1, source_target_pairs={{0,1},{1,2},{2,3},{3,0},{4,5},{5,6},{6,7},{7,4},{8,9},{9,10},{10,1... | collective-permute-start | bytes 1568 | tf_op jit(solution)/shard_map/ppermute | solution.py:22
  243.6 19.7 %copy-start = (f32[4,40,24,2]{3,1,2,0:T(8,128)S(1)}, f32[4,40,24,2]{3,1,2,0:T(8,128)}, u32[]{:S(2)}) copy-start(f32[4,40,24,2]{3,1,2,0:T(8,128)} %copy.9) | copy-start | bytes 92164
  243.6 19.7 %copy-start.1 = (f32[4,40,24,2]{3,1,2,0:T(8,128)S(1)}, f32[4,40,24,2]{3,1,2,0:T(8,128)}, u32[]{:S(2)}) copy-start(f32[4,40,24,2]{3,1,2,0:T(8,128)} %copy.11) | copy-start | bytes 92164
  245.2 9.7 %collective-permute-start.23 = (f32[4,40,2,132]{3,1,2,0:T(8,128)S(1)}, f32[4,40,2,132]{3,1,2,0:T(8,128)S(1)}, u32[]{:S(2)}, u32[]{:S(2)}) collective-permute-start(f32[4,40,2,132]{3,1,2,0:T(8,128)S(1)} %get-tuple-element.40), channel_id=1, source_target_pairs={{1,0},{2,1},{3,2},{0,3},{5,4},{6,5},{7,6},{4,7},{9,8},{10,9},{11,1... | collective-permute-start | bytes 506888 | tf_op jit(solution)/shard_map/ppermute | solution.py:24
  246.8 15.7 %collective-permute-start.22 = (f32[4,40,2,132]{3,1,2,0:T(8,128)S(1)}, f32[4,40,2,132]{3,1,2,0:T(8,128)S(1)}, u32[]{:S(2)}, u32[]{:S(2)}) collective-permute-start(f32[4,40,2,132]{3,1,2,0:T(8,128)S(1)} %get-tuple-element.41), channel_id=1, source_target_pairs={{0,1},{1,2},{2,3},{3,0},{4,5},{5,6},{6,7},{7,4},{8,9},{9,10},{10,1... | collective-permute-start | bytes 506888 | tf_op jit(solution)/shard_map/ppermute | solution.py:22
  255.0 7.6 %copy-start.5 = (f32[4,40,2,132]{3,1,2,0:T(8,128)}, f32[4,40,2,132]{3,1,2,0:T(8,128)S(1)}, u32[]{:S(2)}) copy-start(f32[4,40,2,132]{3,1,2,0:T(8,128)S(1)} %collective-permute-done.23) | copy-start | bytes 506884
  270.5 11.5 %copy-start.6 = (f32[4,40,2,132]{3,1,2,0:T(8,128)S(1)}, f32[4,40,2,132]{3,1,2,0:T(8,128)}, u32[]{:S(2)}) copy-start(f32[4,40,2,132]{3,1,2,0:T(8,128)} %copy-done.5) | copy-start | bytes 506884
  270.5 11.5 %copy-start.8 = (f32[4,40,2,132]{3,1,2,0:T(8,128)S(1)}, f32[4,40,2,132]{3,1,2,0:T(8,128)}, u32[]{:S(2)}) copy-start(f32[4,40,2,132]{3,1,2,0:T(8,128)} %copy-done.7) | copy-start | bytes 506884
  270.5 11.5 %copy-start.9 = (f32[40,24,128]{2,0,1:T(8,128)S(1)}, f32[40,24,128]{2,0,1:T(8,128)}, u32[]{:S(2)}) copy-start(f32[40,24,128]{2,0,1:T(8,128)} %get-tuple-element.50) | copy-start | bytes 1474564
  (8 other events, 23.3 us)
where the time goes:
time: 299 us; the launch traced here: 298 us
  blocking collectives  153 us (51%)
  other arithmetic  41.4 us (14%)
  waiting for transfers between devices  37 us (12%)
  starting transfers between devices  32.7 us (11%)
  local copies, waits for them, and re-layouts  19.4 us (6%)
  between operations  14.1 us (5%)
    psum x4, blocking collectives, paired_totals(): lax.psum((jnp.sum(trim_rims(residual * search, width)), jnp.sum(trim_rims...  153 us
    ppermute x12, starting transfers between devices, with_halo(): lax.ppermute(head, axis, [((i + 1) % count, i) for i in range(count)])  28.2 us
    ppermute x12, waiting for transfers between devices, with_halo(): lax.ppermute(tail, axis, [(i, (i + 1) % count) for i in range(count)])  25.7 us
    mul x1, other arithmetic, tendency_of(): return trim_rims(active_wide, 2) * (-flux - viscosity * smoothed)  12.6 us
    sub x1, other arithmetic, laplace(): return east_part - west_part + north_part - south_part  11.5 us
    ppermute x12, waiting for transfers between devices, with_halo(): lax.ppermute(head, axis, [((i + 1) % count, i) for i in range(count)])  11.3 us
    unnamed x36, local copies, waits for them, and re-layouts  9.51 us
  transfers between devices with their start and end apart: 24, of which 13 were waited for; matrix products, arithmetic and copies ran while one was open for 7% of the time, Pallas kernels for 0%

commit v1 on v0

v1 whole, which is shorter than its diff:
```python
import functools

import jax
import jax.numpy as jnp
from jax import lax
from jax.experimental import pallas as pl
from jax.experimental.pallas import tpu as pltpu
from jax.sharding import PartitionSpec as P

ITERS = 4
damping = 0.05
viscosity = 0.02
LEVEL_BLOCK = 8
HALF = 64


def lane_iota(shape):
    return lax.broadcasted_iota(jnp.int32, shape, 1)


def pick_block(levels):
    return LEVEL_BLOCK if levels % LEVEL_BLOCK == 0 else 1


def pack_kernel(force_ref, sea_ref, count_ref, state_ref, north_ref, south_ref, pair_ref, cols_ref, *, levels):
    step = pl.program_id(0)
    fields, block, height, width = state_ref.shape

    @pl.when(step == 0)
    def _():
        sea = sea_ref[...].astype(jnp.float32)
        wet = sea * count_ref[...].astype(jnp.float32)
        forcing = sea * force_ref[...]
        half = height // 2
        for n in range(half):
            rows = slice(2 * n, 2 * n + 2)
            for ref, start in ((north_ref, fields * levels), (south_ref, fields * levels), (pair_ref, 0)):
                ref[start + n] = forcing[rows]
                ref[start + half + n] = wet[rows]
        cols_ref[...] = jnp.zeros(cols_ref.shape, jnp.float32)

    lane = lane_iota((height, width))
    edges = (0, 1, width - 2, width - 1)
    held = [[cols_ref[c, p] for p in range(fields // 2)] for c in range(4)]
    for kk in range(block):
        level = step * block + kk
        for f in range(fields):
            x = state_ref[f, kk]
            north_ref[f * levels + level] = x[height - 2 :]
            south_ref[f * levels + level] = x[:2]
            spot = (f % 2) * HALF + level
            mine = lane == spot
            for c, edge in enumerate(edges):
                moved = pltpu.roll(x, lax.rem(spot + (width - edge), width), 1)
                held[c][f // 2] = jnp.where(mine, moved, held[c][f // 2])
    for c in range(4):
        for p in range(fields // 2):
            cols_ref[c, p] = held[c][p]


def middle_kernel(*refs, levels, fields, lats):
    place_ref, cols_ref, own_ref = refs[:3]
    others = refs[3 : 3 + lats - 1]
    halo_ref, wide_ref, west_ref, east_ref, grid_ref, tall = refs[3 + lats - 1 :]
    height, width = cols_ref.shape[2:]
    half = height // 2
    base = fields * levels
    north, south = others[0], others[lats - 2]
    for b in range(lats):
        source = own_ref if b == 0 else others[b - 1]
        start = base if b in (1, lats - 1) else 0
        for n in range(height):
            grid_ref[b * 2 * height + 2 * n : b * 2 * height + 2 * n + 2] = source[start + n]
    lat = place_ref[0]
    wide_ref[:height] = grid_ref[height : 2 * height]
    wide_ref[height:] = jnp.zeros((8, width), jnp.float32)

    @pl.when(lat < lats - 1)
    def _():
        wide_ref[height : height + 2] = north[base + half]

    @pl.when(lat > 0)
    def _():
        wide_ref[height + 6 : height + 8] = south[base + height - 1]

    lane8 = lane_iota((8, width))
    near = [[jnp.zeros((8, width), jnp.float32) for _ in range(fields // 2)] for _ in range(2)]
    empty = jnp.zeros((4, width), jnp.float32)
    for f in range(fields):
        for k in range(levels):
            n = f * levels + k
            halo_ref[f, k, 0:2] = north[n]
            halo_ref[f, k, 2:6] = empty
            halo_ref[f, k, 6:8] = south[n]
    for f in range(fields):
        for k in range(levels):
            x = halo_ref[f, k]
            spot = (f % 2) * HALF + k
            for c, edge in enumerate((0, width - 1)):
                near[c][f // 2] = jnp.where(lane8 == spot, pltpu.roll(x, (spot - edge) % width, 1), near[c][f // 2])
    tall_rows = height + 8
    wide = wide_ref[...]
    lane_tall = lane_iota((tall_rows, width))
    for out_ref, c_near, c_far, edge_near, edge_far, slot in (
        (west_ref, 0, 1, 0, 1, 0),
        (east_ref, 3, 2, width - 1, width - 2, 1),
    ):
        for p in range(fields // 2):
            tall[:height] = cols_ref[c_near, p]
            tall[height:] = near[slot][p]
            value = tall[...]
            tall[:height] = cols_ref[c_far, p]
            tall[height:] = jnp.zeros((8, width), jnp.float32)
            value_far = tall[...]
            if p == 0:
                value = jnp.where(lane_tall == levels, pltpu.roll(wide, (levels - edge_near) % width, 1), value)
                value_far = jnp.where(lane_tall == levels, pltpu.roll(wide, (levels - edge_far) % width, 1), value_far)
            out_ref[p * tall_rows : (p + 1) * tall_rows] = value
            q = fields // 2 + p
            out_ref[q * tall_rows : (q + 1) * tall_rows] = value_far
        out_ref[2 * (fields // 2) * tall_rows :] = grid_ref[...]


def tendency_kernel(state_ref, halo_ref, wide_ref, own_w_ref, own_e_ref, got_w_ref, got_e_ref, out_ref, faces, edge_lap, *, levels):
    step = pl.program_id(0)
    fields, block, height, width = state_ref.shape
    rows = height + 8
    pairs = fields // 2
    lane = lane_iota((rows, width))
    last, first = lane == width - 1, lane == 0

    def part(ref, far, p):
        q = (pairs if far else 0) + p
        return ref[q * rows : (q + 1) * rows]

    def up(x):
        return pltpu.roll(x, rows - 1, 0)

    def down(x):
        return pltpu.roll(x, 1, 0)

    @pl.when(step == 0)
    def _():
        wide = wide_ref[...]
        east = jnp.where(last, pltpu.roll(part(got_e_ref, False, 0), width - 1 - levels, 1), pltpu.roll(wide, width - 1, 1))
        west = jnp.where(first, pltpu.roll(part(got_w_ref, False, 0), width - levels, 1), pltpu.roll(wide, 1, 1))
        for n, other in enumerate((east, west, up(wide), down(wide))):
            faces[n] = jnp.minimum(wide, other)
        depth_at = lax.rem(lane, HALF).astype(jnp.float32)
        for side, (got, own, sign) in enumerate(((got_w_ref, own_w_ref, 1.0), (got_e_ref, own_e_ref, -1.0))):
            wet_near, wet_far, wet_own = (
                jnp.broadcast_to(part(ref, far, 0)[:, levels : levels + 1], (rows, width))
                for ref, far in ((got, False), (got, True), (own, False))
            )
            masks = [depth_at < jnp.minimum(wet_near, other) for other in (wet_own, wet_far, up(wet_near), down(wet_near))]
            for p in range(pairs):
                here, beyond, inner = part(got, False, p), part(got, True, p), part(own, False, p)
                total = jnp.zeros((rows, width), jnp.float32)
                for mask, other in zip(masks, (inner, beyond, up(here), down(here))):
                    total = total + jnp.where(mask, other - here, 0.0)
                edge_lap[side, p] = total

    wide = wide_ref[...]
    low = slice(0, height)
    for kk in range(block):
        level = step * block + kk
        depth = level.astype(jnp.float32)
        on_e, on_w, on_n, on_s = (depth < faces[n] for n in range(4))
        here_on = depth < wide[low]
        around = []
        for f in range(fields):
            x = jnp.concatenate([state_ref[f, kk], halo_ref[f, kk]], axis=0)
            spot = (f % 2) * HALF + level
            p = f // 2
            east = jnp.where(last, pltpu.roll(part(got_e_ref, False, p), width - 1 - spot, 1), pltpu.roll(x, width - 1, 1))
            west = jnp.where(first, pltpu.roll(part(got_w_ref, False, p), lax.rem(width - spot, width), 1), pltpu.roll(x, 1, 1))
            around.append((x, east, west, up(x), down(x)))
        u, v = around[2], around[3]
        mask_low = [m[low] for m in (on_e, on_w, on_n, on_s)]
        speed = [
            jnp.where(mask_low[0], 0.25 * (u[0][low] + u[1][low]), 0.0),
            jnp.where(mask_low[1], 0.25 * (u[0][low] + u[2][low]), 0.0),
            jnp.where(mask_low[2], 0.25 * (v[0][low] + v[3][low]), 0.0),
            jnp.where(mask_low[3], 0.25 * (v[0][low] + v[4][low]), 0.0),
        ]
        for f in range(fields):
            x, east, west, north, south = around[f]
            spot = (f % 2) * HALF + level
            p = f // 2
            lap = (
                jnp.where(on_e, east - x, 0.0)
                - jnp.where(on_w, x - west, 0.0)
                + jnp.where(on_n, north - x, 0.0)
                - jnp.where(on_s, x - south, 0.0)
            )
            inner = lap[low]
            lap_e = jnp.where(last[low], pltpu.roll(edge_lap[1, p][low], width - 1 - spot, 1), pltpu.roll(inner, width - 1, 1))
            lap_w = jnp.where(first[low], pltpu.roll(edge_lap[0, p][low], lax.rem(width - spot, width), 1), pltpu.roll(inner, 1, 1))
            lap_n, lap_s = up(lap)[low], down(lap)[low]
            second = (
                jnp.where(mask_low[0], lap_e - inner, 0.0)
                - jnp.where(mask_low[1], inner - lap_w, 0.0)
                + jnp.where(mask_low[2], lap_n - inner, 0.0)
                - jnp.where(mask_low[3], inner - lap_s, 0.0)
            )
            q = x[low]
            flux = (
                speed[0] * (q + east[low])
                - speed[1] * (q + west[low])
                + speed[2] * (q + north[low])
                - speed[3] * (q + south[low])
            )
            out_ref[f, kk] = jnp.where(here_on, -flux - viscosity * second, 0.0)


def solve_kernel(*refs, levels, lats, lons, height, width):
    place_ref = refs[0]
    sources = refs[1 : 1 + lons]
    height_ref, residual_ref = refs[1 + lons : 3 + lons]
    depth_ref, east_ref, west_ref, north_ref, south_ref, diag_ref, r_ref, p_ref = refs[3 + lons :]
    tall, broad = lats * height, lons * width
    for d, source in enumerate(sources):
        start = source.shape[0] - lats * 2 * height
        for b in range(lats):
            at = start + b * 2 * height
            block = (slice(b * height, (b + 1) * height), slice(d * width, (d + 1) * width))
            r_ref[block] = source[at : at + height]
            depth_ref[block] = source[at + height : at + 2 * height] / levels

    def to_east(x):
        return pltpu.roll(x, broad - 1, 1)

    def to_west(x):
        return pltpu.roll(x, 1, 1)

    def to_north(x):
        return pltpu.roll(x, tall - 1, 0)

    def to_south(x):
        return pltpu.roll(x, 1, 0)

    depth = depth_ref[...]
    row = lax.rem(lax.broadcasted_iota(jnp.int32, (tall, broad), 0) + place_ref[0] * height, tall)
    east_ref[...] = jnp.minimum(depth, to_east(depth))
    west_ref[...] = jnp.minimum(depth, to_west(depth))
    north_ref[...] = jnp.where(row == tall - 1, 0.0, jnp.minimum(depth, to_north(depth)))
    south_ref[...] = jnp.where(row == 0, 0.0, jnp.minimum(depth, to_south(depth)))
    diag_ref[...] = damping + east_ref[...] + west_ref[...] + north_ref[...] + south_ref[...]
    depth_ref[...] = 1.0 / diag_ref[...]
    inverse_ref = depth_ref
    search = r_ref[...] * inverse_ref[...]
    p_ref[...] = search

    def total(x):
        return jnp.sum(jnp.sum(x, axis=0, keepdims=True), axis=1, keepdims=True)

    product = total(r_ref[...] * search)

    def advance(product, answer):
        p = p_ref[...]
        image = (
            diag_ref[...] * p
            - east_ref[...] * to_east(p)
            - west_ref[...] * to_west(p)
            - north_ref[...] * to_north(p)
            - south_ref[...] * to_south(p)
        )
        alpha = product / total(p * image)
        answer = answer + alpha * p_ref[:height, :width]
        r_ref[...] = r_ref[...] - alpha * image
        return answer

    def step(_, carry):
        product, answer = carry
        answer = advance(product, answer)
        search = r_ref[...] * inverse_ref[...]
        new = total(r_ref[...] * search)
        p_ref[...] = search + (new / product) * p_ref[...]
        return new, answer

    product, answer = lax.fori_loop(0, ITERS - 1, step, (product, jnp.zeros((height, width), jnp.float32)))
    height_ref[...] = advance(product, answer)
    residual_ref[...] = r_ref[:height, :width]


def shifted(x, axis, distance):
    count = lax.axis_size(axis)
    return lax.ppermute(x, axis, [((i + distance) % count, i) for i in range(count)])


def per_device(surface_forcing, sea_mask, level_count, state):
    fields, levels, height, width = state.shape
    lats, lons = lax.axis_size("lat"), lax.axis_size("lon")
    block = pick_block(levels)
    f32 = jnp.float32
    pairs = fields // 2
    rows = height + 8
    whole = lambda shape: pl.BlockSpec(shape, lambda i: (0,) * len(shape))
    message = (fields * levels + height, 2, width)
    north_msg, south_msg, pair, cols = pl.pallas_call(
        functools.partial(pack_kernel, levels=levels),
        grid=(levels // block,),
        in_specs=[whole((height, width))] * 3 + [pl.BlockSpec((fields, block, height, width), lambda i: (0, i, 0, 0))],
        out_specs=[whole(message), whole(message), whole((height, 2, width)), whole((4, pairs, height, width))],
        out_shape=[
            jax.ShapeDtypeStruct(message, f32),
            jax.ShapeDtypeStruct(message, f32),
            jax.ShapeDtypeStruct((height, 2, width), f32),
            jax.ShapeDtypeStruct((4, pairs, height, width), f32),
        ],
        name="pack",
    )(surface_forcing, sea_mask, level_count, state)

    place = lax.axis_index("lat").astype(jnp.int32)[None]
    from_lat = [
        shifted(south_msg if b == 1 else north_msg if b == lats - 1 else pair, "lat", b) for b in range(1, lats)
    ]
    smem = pl.BlockSpec(memory_space=pltpu.SMEM)
    vmem = pl.BlockSpec(memory_space=pltpu.VMEM)
    strip = 2 * pairs * rows
    cells = lats * 2 * height
    halo, wide, west_msg, east_msg, grid = pl.pallas_call(
        functools.partial(middle_kernel, levels=levels, fields=fields, lats=lats),
        in_specs=[smem] + [vmem] * (2 + lats - 1),
        out_specs=[vmem] * 5,
        out_shape=[
            jax.ShapeDtypeStruct((fields, levels, 8, width), f32),
            jax.ShapeDtypeStruct((rows, width), f32),
            jax.ShapeDtypeStruct((strip + cells, width), f32),
            jax.ShapeDtypeStruct((strip + cells, width), f32),
            jax.ShapeDtypeStruct((cells, width), f32),
        ],
        scratch_shapes=[pltpu.VMEM((rows, width), f32)],
        name="middle",
    )(place, cols, pair, *from_lat)

    order = [1, lons - 1] + list(range(2, lons - 1))
    got = {d: shifted(west_msg if d == 1 else east_msg if d == lons - 1 else grid, "lon", d) for d in order}
    tendency = pl.pallas_call(
        functools.partial(tendency_kernel, levels=levels),
        grid=(levels // block,),
        in_specs=[
            pl.BlockSpec((fields, block, height, width), lambda i: (0, i, 0, 0)),
            pl.BlockSpec((fields, block, 8, width), lambda i: (0, i, 0, 0)),
            whole((rows, width)),
        ]
        + [whole((strip, width))] * 4,
        out_specs=pl.BlockSpec((fields, block, height, width), lambda i: (0, i, 0, 0)),
        out_shape=jax.ShapeDtypeStruct(state.shape, f32),
        scratch_shapes=[pltpu.VMEM((4, rows, width), f32), pltpu.VMEM((2, pairs, rows, width), f32)],
        cost_estimate=pl.CostEstimate(flops=100 * state.size, bytes_accessed=9 * state.size, transcendentals=0),
        name="tendency",
    )(state, halo, wide, west_msg, east_msg, got[lons - 1], got[1])

    field = pltpu.VMEM((lats * height, lons * width), f32)
    surface, residual = pl.pallas_call(
        functools.partial(solve_kernel, levels=levels, lats=lats, lons=lons, height=height, width=width),
        in_specs=[smem] + [vmem] * lons,
        out_specs=[vmem] * 2,
        out_shape=[jax.ShapeDtypeStruct((height, width), f32)] * 2,
        scratch_shapes=[field] * 8,
        name="solve",
    )(place, grid, *[got[d] for d in range(1, lons)])
    return surface, residual, tendency


def solution(mesh):
    return jax.shard_map(
        per_device,
        mesh=mesh,
        in_specs=(P("lat", "lon"), P("lat", "lon"), P("lat", "lon"), P(None, None, "lat", "lon")),
        out_specs=(P("lat", "lon"), P("lat", "lon"), P(None, None, "lat", "lon")),
        check_vma=False,
    )
```

time: 299 us -> 48 us (0.16)
  blocking collectives: 153 us -> 0 us
  other arithmetic: 41.4 us -> 0 us
  waiting for transfers between devices: 37 us -> 11.4 us
  Pallas kernels: 0 us -> 21.2 us
  starting transfers between devices: 32.7 us -> 12.3 us
  local copies, waits for them, and re-layouts: 19.4 us -> 2.16 us
  between operations: 14.1 us -> 0.71 us
    psum x4 -> x0, blocking collectives: 153 us -> none  [paired_totals(): lax.psum((jnp.sum(trim_rims(residual * search, width)), jnp.sum(trim_rims...]
    ppermute x24 -> x10, waiting for transfers between devices: 37 us -> 11.4 us  [shifted(): lax.ppermute(x, axis, [((i + distance) % count, i) for i in range(count)])]
    pallas_call x0 -> x4, Pallas kernels: none -> 21.2 us  [the longest x1 8.46 us: per_device(): pl.pallas_call(functools.partial(tendency_kernel, levels=levels), grid=(l...]
    ppermute x24 -> x10, starting transfers between devices: 32.7 us -> 12.3 us  [shifted(): lax.ppermute(x, axis, [((i + distance) % count, i) for i in range(count)])]
    mul x5 -> x0, other arithmetic: 17.6 us -> none  [the longest x1 12.6 us: tendency_of(): return trim_rims(active_wide, 2) * (-flux - viscosity * smoothed)]
    sub x2 -> x0, other arithmetic: 12.1 us -> none  [the longest x1 11.5 us: laplace(): return east_part - west_part + north_part - south_part]
    unnamed x36 -> x20, local copies, waits for them, and re-layouts: 9.51 us -> 2.16 us
    ppermute x2 -> x0, local copies, waits for them, and re-layouts: 4.9 us -> none  [the longest x1 2.91 us: with_halo(): lax.ppermute(tail, axis, [(i, (i + 1) % count) for i in range(count)])]
  transfers between devices with their start and end apart: 24 -> 10, of which waited for: 13 -> 4; matrix products, arithmetic and copies ran while one was open for 7% -> 0% of each run, Pallas kernels for 0% -> 18%
where the time goes in v1:
time: 48 us; the launch traced here: 47.7 us
  Pallas kernels  21.2 us (44%)
  starting transfers between devices  12.3 us (26%)
  waiting for transfers between devices  11.4 us (24%)
  local copies, waits for them, and re-layouts  2.16 us (4%)
  between operations  0.71 us (1%)
    ppermute x10, starting transfers between devices, shifted(): lax.ppermute(x, axis, [((i + distance) % count, i) for i in range(count)])  12.3 us
    ppermute x10, waiting for transfers between devices, shifted(): lax.ppermute(x, axis, [((i + distance) % count, i) for i in range(count)])  11.4 us
    pallas_call x1, Pallas kernels, per_device(): pl.pallas_call(functools.partial(tendency_kernel, levels=levels), grid=(l...  8.46 us
    pallas_call x1, Pallas kernels, per_device(): pl.pallas_call(functools.partial(pack_kernel, levels=levels), grid=(level...  5.2 us
    pallas_call x1, Pallas kernels, per_device(): pl.pallas_call(functools.partial(solve_kernel, levels=levels, lats=lats,...  5.02 us
    pallas_call x1, Pallas kernels, per_device(): pl.pallas_call(functools.partial(middle_kernel, levels=levels, fields=fie...  2.54 us
    unnamed x20, local copies, waits for them, and re-layouts  2.16 us
  transfers between devices with their start and end apart: 10, of which 4 were waited for; matrix products, arithmetic and copies ran while one was open for 0% of the time, Pallas kernels for 18%

profile of v1, /device:TPU:0, one launch (start us, length us, event | category | flops | bytes accessed | tf_op | source)
XLA Modules:
  0.0 47.7 jit_solution(17378752190101596792)
XLA Ops:
  0.6 5.2 %pack.1 = (f32[184,2,128]{2,1,0:T(2,128)}, f32[184,2,128]{2,1,0:T(2,128)}, f32[24,2,128]{2,1,0:T(2,128)}, f32[4,2,24,128]{3,2,1,0:T(8,128)}) custom-call(f32[24,128]{1,0:T(8,128)} %force_ref.1, s32[24,128]{1,0:T(8,128)} %sea_ref.1, s32[24,128]{1,0:T(8,128)} %count_ref.1, f32[4,40,24,128]{3,2,1,0:T(8,128)} %state_ref.3), custom_call_target="tpu_custom_call" | custom-call | tf_op jit(solution)/shard_map/pack/pallas_call | solution.py:300
  5.8 5.1 %collective-permute-start = (f32[184,2,128]{2,1,0:T(2,128)}, f32[184,2,128]{2,1,0:T(2,128)S(1)}, u32[]{:S(2)}, u32[]{:S(2)}) collective-permute-start(f32[184,2,128]{2,1,0:T(2,128)} %get-tuple-element.16), channel_id=1, source_target_pairs={{1,0},{2,1},{3,2},{0,3},{5,4},{6,5},{7,6},{4,7},{9,8},{10,9},{11,1... | collective-permute-start | bytes 565256 | tf_op jit(solution)/shard_map/ppermute | solution.py:288
  10.9 0.0 collective-permute-start.2
  10.9 1.0 %collective-permute-start.1 = (f32[24,2,128]{2,1,0:T(2,128)}, f32[24,2,128]{2,1,0:T(2,128)S(1)}, u32[]{:S(2)}, u32[]{:S(2)}) collective-permute-start(f32[24,2,128]{2,1,0:T(2,128)} %get-tuple-element.15.refs_2_), channel_id=1, source_target_pairs={{2,0},{3,1},{0,2},{1,3},{6,4},{7,5},{4,6},{5,7},{10,8},{11,9},{8,1... | collective-permute-start | bytes 73736 | tf_op jit(solution)/shard_map/ppermute | solution.py:288
  11.9 7.8 %collective-permute-done.1.refs_4_ = f32[24,2,128]{2,1,0:T(2,128)S(1)} collective-permute-done((f32[24,2,128]{2,1,0:T(2,128)}, f32[24,2,128]{2,1,0:T(2,128)S(1)}, u32[]{:S(2)}, u32[]{:S(2)}) %collective-permute-start.1) | collective-permute-done | bytes 24608 | tf_op jit(solution)/shard_map/ppermute | solution.py:288
  19.7 0.0 collective-permute-done.refs_3_
  19.7 0.6 %collective-permute-done.2.refs_5_ = f32[184,2,128]{2,1,0:T(2,128)S(1)} collective-permute-done((f32[184,2,128]{2,1,0:T(2,128)}, f32[184,2,128]{2,1,0:T(2,128)S(1)}, u32[]{:S(2)}, u32[]{:S(2)}) %collective-permute-start.2) | collective-permute-done | bytes 188448 | tf_op jit(solution)/shard_map/ppermute | solution.py:288
  20.3 0.0 copy-done.9
  20.3 0.1 copy-done.2
  20.4 0.6 %copy-done.3 = f32[184,2,128]{2,1,0:T(2,128)} copy-done((f32[184,2,128]{2,1,0:T(2,128)}, f32[184,2,128]{2,1,0:T(2,128)S(1)}, u32[]{:S(2)}) %copy-start.3) | copy-done | bytes 188440
  21.0 2.5 %middle.1 = (f32[4,40,8,128]{3,2,1,0:T(8,128)}, f32[32,128]{1,0:T(8,128)}, f32[320,128]{1,0:T(8,128)}, f32[320,128]{1,0:T(8,128)}, f32[192,128]{1,0:T(8,128)}) custom-call(s32[1]{0:T(128)} %bitcast.refs_0_, f32[4,2,24,128]{3,2,1,0:T(8,128)} %get-tuple-element.14.refs_1_, f32[24,2,128]{2,1,0:T(2,128)} %get-tuple-element.15.refs_2_, f32[184,2,128]{2,1,0:T(2,128)} %copy-done.2, ...), custom_call_target="tpu_custom_call" | custom-call | tf_op jit(solution)/shard_map/middle/pallas_call | solution.py:322
  23.5 1.0 %collective-permute-start.3 = (f32[320,128]{1,0:T(8,128)}, f32[320,128]{1,0:T(8,128)S(1)}, u32[]{:S(2)}, u32[]{:S(2)}) collective-permute-start(f32[320,128]{1,0:T(8,128)} %get-tuple-element.19.own_w_ref), channel_id=1, source_target_pairs={{4,0},{8,4},{12,8},{16,12},{20,16},{24,20},{28,24},{0,28},{5,1},{9... | collective-permute-start | bytes 491528 | tf_op jit(solution)/shard_map/ppermute | solution.py:288
  24.5 0.0 collective-permute-start.9
  24.5 1.0 %collective-permute-start.8 = (f32[192,128]{1,0:T(8,128)}, f32[192,128]{1,0:T(8,128)S(1)}, u32[]{:S(2)}, u32[]{:S(2)}) collective-permute-start(f32[192,128]{1,0:T(8,128)} %get-tuple-element.18.refs_1_), channel_id=1, source_target_pairs={{24,0},{28,4},{0,8},{4,12},{8,16},{12,20},{16,24},{20,28},{25,1},{... | collective-permute-start | bytes 294920 | tf_op jit(solution)/shard_map/ppermute | solution.py:288
  25.5 1.9 %collective-permute-start.7 = (f32[192,128]{1,0:T(8,128)}, f32[192,128]{1,0:T(8,128)S(1)}, u32[]{:S(2)}, u32[]{:S(2)}) collective-permute-start(f32[192,128]{1,0:T(8,128)} %get-tuple-element.18.refs_1_), channel_id=1, source_target_pairs={{20,0},{24,4},{28,8},{0,12},{4,16},{8,20},{12,24},{16,28},{21,1},{... | collective-permute-start | bytes 294920 | tf_op jit(solution)/shard_map/ppermute | solution.py:288
  27.4 0.5 %collective-permute-start.6 = (f32[192,128]{1,0:T(8,128)}, f32[192,128]{1,0:T(8,128)S(1)}, u32[]{:S(2)}, u32[]{:S(2)}) collective-permute-start(f32[192,128]{1,0:T(8,128)} %get-tuple-element.18.refs_1_), channel_id=1, source_target_pairs={{16,0},{20,4},{24,8},{28,12},{0,16},{4,20},{8,24},{12,28},{17,1},{... | collective-permute-start | bytes 294920 | tf_op jit(solution)/shard_map/ppermute | solution.py:288
  28.0 1.4 %collective-permute-done.3.refs_2_.got_e_ref = f32[320,128]{1,0:T(8,128)S(1)} collective-permute-done((f32[320,128]{1,0:T(8,128)}, f32[320,128]{1,0:T(8,128)S(1)}, u32[]{:S(2)}, u32[]{:S(2)}) %collective-permute-start.3) | collective-permute-done | bytes 163872 | tf_op jit(solution)/shard_map/ppermute | solution.py:288
  29.4 1.3 %collective-permute-start.5 = (f32[192,128]{1,0:T(8,128)}, f32[192,128]{1,0:T(8,128)S(1)}, u32[]{:S(2)}, u32[]{:S(2)}) collective-permute-start(f32[192,128]{1,0:T(8,128)} %get-tuple-element.18.refs_1_), channel_id=1, source_target_pairs={{12,0},{16,4},{20,8},{24,12},{28,16},{0,20},{4,24},{8,28},{13,1},{... | collective-permute-start | bytes 294920 | tf_op jit(solution)/shard_map/ppermute | solution.py:288
  30.7 1.5 %collective-permute-done.9.refs_8_.got_w_ref = f32[320,128]{1,0:T(8,128)S(1)} collective-permute-done((f32[320,128]{1,0:T(8,128)}, f32[320,128]{1,0:T(8,128)S(1)}, u32[]{:S(2)}, u32[]{:S(2)}) %collective-permute-start.9) | collective-permute-done | bytes 163872 | tf_op jit(solution)/shard_map/ppermute | solution.py:288
  32.2 0.5 %collective-permute-start.4 = (f32[192,128]{1,0:T(8,128)}, f32[192,128]{1,0:T(8,128)S(1)}, u32[]{:S(2)}, u32[]{:S(2)}) collective-permute-start(f32[192,128]{1,0:T(8,128)} %get-tuple-element.18.refs_1_), channel_id=1, source_target_pairs={{8,0},{12,4},{16,8},{20,12},{24,16},{28,20},{0,24},{4,28},{9,1},{1... | collective-permute-start | bytes 294920 | tf_op jit(solution)/shard_map/ppermute | solution.py:288
  32.7 0.2 copy-done.1
  32.9 8.5 %tendency.1 = f32[4,40,24,128]{3,2,1,0:T(8,128)} custom-call(f32[4,40,24,128]{3,2,1,0:T(8,128)} %state_ref.3, f32[4,40,8,128]{3,2,1,0:T(8,128)} %get-tuple-element.23.halo_ref, f32[32,128]{1,0:T(8,128)} %get-tuple-element.24.wide_ref, f32[320,128]{1,0:T(8,128)} %get-tuple-element.19.own_w_ref, f32[320,128]{1,0:T(8,128)} %get-tuple-element.20.own_e_ref, ...), custom_call_target="tpu_custom_call" | custom-call | flops 49152000 | bytes 4423680 | tf_op jit(solution)/shard_map/tendency/pallas_call | solution.py:339
  41.3 0.0 collective-permute-done.8.refs_7_
  41.3 0.0 collective-permute-done.7.refs_6_
  41.3 0.0 collective-permute-done.6.refs_5_
  41.4 0.0 collective-permute-done.4.refs_3_
  41.4 0.6 %copy-done.4 = f32[192,128]{1,0:T(8,128)} copy-done((f32[192,128]{1,0:T(8,128)}, f32[192,128]{1,0:T(8,128)S(1)}, u32[]{:S(2)}) %copy-start.4) | copy-done | bytes 98328
  42.0 0.0 copy-done.5
  42.0 0.0 copy-done.6
  42.0 0.0 copy-done.7
  42.1 0.6 %copy-done.8 = f32[192,128]{1,0:T(8,128)} copy-done((f32[192,128]{1,0:T(8,128)}, f32[192,128]{1,0:T(8,128)S(1)}, u32[]{:S(2)}) %copy-start.8) | copy-done | bytes 98328
  42.7 5.0 %solve.1 = (f32[24,128]{1,0:T(8,128)}, f32[24,128]{1,0:T(8,128)}) custom-call(s32[1]{0:T(128)} %bitcast.refs_0_, f32[192,128]{1,0:T(8,128)} %get-tuple-element.18.refs_1_, f32[320,128]{1,0:T(8,128)} %copy-done, f32[192,128]{1,0:T(8,128)} %copy-done.8, f32[192,128]{1,0:T(8,128)} %copy-done.7, f32[192,128]{1,0:T(8,128)} %copy-done.6, f32[192,128]{1,0:T(8,128)} %copy-done.5, ...), custom_call_target="tpu_custom_call" | custom-call | tf_op jit(solution)/shard_map/solve/pallas_call | solution.py:356
  (12 shorter events, 0.0 us)
Async XLA Ops:
  5.8 13.9 %collective-permute-start = (f32[184,2,128]{2,1,0:T(2,128)}, f32[184,2,128]{2,1,0:T(2,128)S(1)}, u32[]{:S(2)}, u32[]{:S(2)}) collective-permute-start(f32[184,2,128]{2,1,0:T(2,128)} %get-tuple-element.16), channel_id=1, source_target_pairs={{1,0},{2,1},{3,2},{0,3},{5,4},{6,5},{7,6},{4,7},{9,8},{10,9},{11,1... | collective-permute-start | bytes 565256 | tf_op jit(solution)/shard_map/ppermute | solution.py:288
  10.9 9.4 %collective-permute-start.2 = (f32[184,2,128]{2,1,0:T(2,128)}, f32[184,2,128]{2,1,0:T(2,128)S(1)}, u32[]{:S(2)}, u32[]{:S(2)}) collective-permute-start(f32[184,2,128]{2,1,0:T(2,128)} %get-tuple-element.17), channel_id=1, source_target_pairs={{3,0},{0,1},{1,2},{2,3},{7,4},{4,5},{5,6},{6,7},{11,8},{8,9},{9,10... | collective-permute-start | bytes 565256 | tf_op jit(solution)/shard_map/ppermute | solution.py:288
  10.9 8.8 %collective-permute-start.1 = (f32[24,2,128]{2,1,0:T(2,128)}, f32[24,2,128]{2,1,0:T(2,128)S(1)}, u32[]{:S(2)}, u32[]{:S(2)}) collective-permute-start(f32[24,2,128]{2,1,0:T(2,128)} %get-tuple-element.15.refs_2_), channel_id=1, source_target_pairs={{2,0},{3,1},{0,2},{1,3},{6,4},{7,5},{4,6},{5,7},{10,8},{11,9},{8,1... | collective-permute-start | bytes 73736 | tf_op jit(solution)/shard_map/ppermute | solution.py:288
  19.7 0.6 %copy-start.9 = (f32[24,2,128]{2,1,0:T(2,128)}, f32[24,2,128]{2,1,0:T(2,128)S(1)}, u32[]{:S(2)}) copy-start(f32[24,2,128]{2,1,0:T(2,128)S(1)} %collective-permute-done.1.refs_4_) | copy-start | bytes 73732
  19.7 0.7 %copy-start.2 = (f32[184,2,128]{2,1,0:T(2,128)}, f32[184,2,128]{2,1,0:T(2,128)S(1)}, u32[]{:S(2)}) copy-start(f32[184,2,128]{2,1,0:T(2,128)S(1)} %collective-permute-done.refs_3_) | copy-start | bytes 565252
  20.3 0.7 %copy-start.3 = (f32[184,2,128]{2,1,0:T(2,128)}, f32[184,2,128]{2,1,0:T(2,128)S(1)}, u32[]{:S(2)}) copy-start(f32[184,2,128]{2,1,0:T(2,128)S(1)} %collective-permute-done.2.refs_5_) | copy-start | bytes 565252
  23.5 5.9 %collective-permute-start.3 = (f32[320,128]{1,0:T(8,128)}, f32[320,128]{1,0:T(8,128)S(1)}, u32[]{:S(2)}, u32[]{:S(2)}) collective-permute-start(f32[320,128]{1,0:T(8,128)} %get-tuple-element.19.own_w_ref), channel_id=1, source_target_pairs={{4,0},{8,4},{12,8},{16,12},{20,16},{24,20},{28,24},{0,28},{5,1},{9... | collective-permute-start | bytes 491528 | tf_op jit(solution)/shard_map/ppermute | solution.py:288
  24.5 7.7 %collective-permute-start.9 = (f32[320,128]{1,0:T(8,128)}, f32[320,128]{1,0:T(8,128)S(1)}, u32[]{:S(2)}, u32[]{:S(2)}) collective-permute-start(f32[320,128]{1,0:T(8,128)} %get-tuple-element.20.own_e_ref), channel_id=1, source_target_pairs={{28,0},{0,4},{4,8},{8,12},{12,16},{16,20},{20,24},{24,28},{29,1},{... | collective-permute-start | bytes 491528 | tf_op jit(solution)/shard_map/ppermute | solution.py:288
  24.5 16.8 %collective-permute-start.8 = (f32[192,128]{1,0:T(8,128)}, f32[192,128]{1,0:T(8,128)S(1)}, u32[]{:S(2)}, u32[]{:S(2)}) collective-permute-start(f32[192,128]{1,0:T(8,128)} %get-tuple-element.18.refs_1_), channel_id=1, source_target_pairs={{24,0},{28,4},{0,8},{4,12},{8,16},{12,20},{16,24},{20,28},{25,1},{... | collective-permute-start | bytes 294920 | tf_op jit(solution)/shard_map/ppermute | solution.py:288
  25.5 15.8 %collective-permute-start.7 = (f32[192,128]{1,0:T(8,128)}, f32[192,128]{1,0:T(8,128)S(1)}, u32[]{:S(2)}, u32[]{:S(2)}) collective-permute-start(f32[192,128]{1,0:T(8,128)} %get-tuple-element.18.refs_1_), channel_id=1, source_target_pairs={{20,0},{24,4},{28,8},{0,12},{4,16},{8,20},{12,24},{16,28},{21,1},{... | collective-permute-start | bytes 294920 | tf_op jit(solution)/shard_map/ppermute | solution.py:288
  27.4 13.9 %collective-permute-start.6 = (f32[192,128]{1,0:T(8,128)}, f32[192,128]{1,0:T(8,128)S(1)}, u32[]{:S(2)}, u32[]{:S(2)}) collective-permute-start(f32[192,128]{1,0:T(8,128)} %get-tuple-element.18.refs_1_), channel_id=1, source_target_pairs={{16,0},{20,4},{24,8},{28,12},{0,16},{4,20},{8,24},{12,28},{17,1},{... | collective-permute-start | bytes 294920 | tf_op jit(solution)/shard_map/ppermute | solution.py:288
  29.4 3.3 %copy-start = (f32[320,128]{1,0:T(8,128)}, f32[320,128]{1,0:T(8,128)S(1)}, u32[]{:S(2)}) copy-start(f32[320,128]{1,0:T(8,128)S(1)} %collective-permute-done.3.refs_2_.got_e_ref) | copy-start | bytes 491524
  29.4 12.0 %collective-permute-start.5 = (f32[192,128]{1,0:T(8,128)}, f32[192,128]{1,0:T(8,128)S(1)}, u32[]{:S(2)}, u32[]{:S(2)}) collective-permute-start(f32[192,128]{1,0:T(8,128)} %get-tuple-element.18.refs_1_), channel_id=1, source_target_pairs={{12,0},{16,4},{20,8},{24,12},{28,16},{0,20},{4,24},{8,28},{13,1},{... | collective-permute-start | bytes 294920 | tf_op jit(solution)/shard_map/ppermute | solution.py:288
  32.2 0.7 %copy-start.1 = (f32[320,128]{1,0:T(8,128)}, f32[320,128]{1,0:T(8,128)S(1)}, u32[]{:S(2)}) copy-start(f32[320,128]{1,0:T(8,128)S(1)} %collective-permute-done.9.refs_8_.got_w_ref) | copy-start | bytes 491524
  32.2 9.2 %collective-permute-start.4 = (f32[192,128]{1,0:T(8,128)}, f32[192,128]{1,0:T(8,128)S(1)}, u32[]{:S(2)}, u32[]{:S(2)}) collective-permute-start(f32[192,128]{1,0:T(8,128)} %get-tuple-element.18.refs_1_), channel_id=1, source_target_pairs={{8,0},{12,4},{16,8},{20,12},{24,16},{28,20},{0,24},{4,28},{9,1},{1... | collective-permute-start | bytes 294920 | tf_op jit(solution)/shard_map/ppermute | solution.py:288
  41.3 0.6 %copy-start.4 = (f32[192,128]{1,0:T(8,128)}, f32[192,128]{1,0:T(8,128)S(1)}, u32[]{:S(2)}) copy-start(f32[192,128]{1,0:T(8,128)S(1)} %collective-permute-done.8.refs_7_) | copy-start | bytes 294916
  41.3 0.7 %copy-start.5 = (f32[192,128]{1,0:T(8,128)}, f32[192,128]{1,0:T(8,128)S(1)}, u32[]{:S(2)}) copy-start(f32[192,128]{1,0:T(8,128)S(1)} %collective-permute-done.7.refs_6_) | copy-start | bytes 294916
  41.4 0.7 %copy-start.6 = (f32[192,128]{1,0:T(8,128)}, f32[192,128]{1,0:T(8,128)S(1)}, u32[]{:S(2)}) copy-start(f32[192,128]{1,0:T(8,128)S(1)} %collective-permute-done.6.refs_5_) | copy-start | bytes 294916
  41.4 0.7 %copy-start.7 = (f32[192,128]{1,0:T(8,128)}, f32[192,128]{1,0:T(8,128)S(1)}, u32[]{:S(2)}) copy-start(f32[192,128]{1,0:T(8,128)S(1)} %collective-permute-done.5.refs_4_) | copy-start | bytes 294916
  42.1 0.6 %copy-start.8 = (f32[192,128]{1,0:T(8,128)}, f32[192,128]{1,0:T(8,128)S(1)}, u32[]{:S(2)}) copy-start(f32[192,128]{1,0:T(8,128)S(1)} %collective-permute-done.4.refs_3_) | copy-start | bytes 294916

commit v2 on v1

--- a/solution.py
+++ b/solution.py
@@ -22,7 +22,9 @@
     return LEVEL_BLOCK if levels % LEVEL_BLOCK == 0 else 1
 
 
-def pack_kernel(force_ref, sea_ref, count_ref, state_ref, north_ref, south_ref, pair_ref, cols_ref, *, levels):
+def pack_kernel(
+    force_ref, sea_ref, count_ref, state_ref, up_ref, down_ref, north_ref, south_ref, pair_ref, cols_ref, *, levels
+):
     step = pl.program_id(0)
     fields, block, height, width = state_ref.shape
 
@@ -34,9 +36,9 @@
         half = height // 2
         for n in range(half):
             rows = slice(2 * n, 2 * n + 2)
-            for ref, start in ((north_ref, fields * levels), (south_ref, fields * levels), (pair_ref, 0)):
-                ref[start + n] = forcing[rows]
-                ref[start + half + n] = wet[rows]
+            for ref in (north_ref, south_ref, pair_ref):
+                ref[n] = forcing[rows]
+                ref[half + n] = wet[rows]
         cols_ref[...] = jnp.zeros(cols_ref.shape, jnp.float32)
 
     lane = lane_iota((height, width))
@@ -46,8 +48,8 @@
         level = step * block + kk
         for f in range(fields):
             x = state_ref[f, kk]
-            north_ref[f * levels + level] = x[height - 2 :]
-            south_ref[f * levels + level] = x[:2]
+            up_ref[f, kk] = x[height - 2 :]
+            down_ref[f, kk] = x[:2]
             spot = (f % 2) * HALF + level
             mine = lane == spot
             for c, edge in enumerate(edges):
@@ -56,48 +58,35 @@
     for c in range(4):
         for p in range(fields // 2):
             cols_ref[c, p] = held[c][p]
+    for slot, c in enumerate((0, 3)):
+        for p in range(fields // 2):
+            north_ref[height + slot, p : p + 1] = held[c][p][height - 1 :]
+            south_ref[height + slot, p : p + 1] = held[c][p][:1]
 
 
 def middle_kernel(*refs, levels, fields, lats):
     place_ref, cols_ref, own_ref = refs[:3]
     others = refs[3 : 3 + lats - 1]
-    halo_ref, wide_ref, west_ref, east_ref, grid_ref, tall = refs[3 + lats - 1 :]
+    wide_ref, west_ref, east_ref, grid_ref, tall = refs[3 + lats - 1 :]
     height, width = cols_ref.shape[2:]
     half = height // 2
-    base = fields * levels
     north, south = others[0], others[lats - 2]
     for b in range(lats):
         source = own_ref if b == 0 else others[b - 1]
-        start = base if b in (1, lats - 1) else 0
         for n in range(height):
-            grid_ref[b * 2 * height + 2 * n : b * 2 * height + 2 * n + 2] = source[start + n]
+            grid_ref[b * 2 * height + 2 * n : b * 2 * height + 2 * n + 2] = source[n]
     lat = place_ref[0]
     wide_ref[:height] = grid_ref[height : 2 * height]
     wide_ref[height:] = jnp.zeros((8, width), jnp.float32)
 
     @pl.when(lat < lats - 1)
     def _():
-        wide_ref[height : height + 2] = north[base + half]
+        wide_ref[height : height + 2] = north[half]
 
     @pl.when(lat > 0)
     def _():
-        wide_ref[height + 6 : height + 8] = south[base + height - 1]
-
-    lane8 = lane_iota((8, width))
-    near = [[jnp.zeros((8, width), jnp.float32) for _ in range(fields // 2)] for _ in range(2)]
-    empty = jnp.zeros((4, width), jnp.float32)
-    for f in range(fields):
-        for k in range(levels):
-            n = f * levels + k
-            halo_ref[f, k, 0:2] = north[n]
-            halo_ref[f, k, 2:6] = empty
-            halo_ref[f, k, 6:8] = south[n]
-    for f in range(fields):
-        for k in range(levels):
-            x = halo_ref[f, k]
-            spot = (f % 2) * HALF + k
-            for c, edge in enumerate((0, width - 1)):
-                near[c][f // 2] = jnp.where(lane8 == spot, pltpu.roll(x, (spot - edge) % width, 1), near[c][f // 2])
+        wide_ref[height + 6 : height + 8] = south[height - 1]
+
     tall_rows = height + 8
     wide = wide_ref[...]
     lane_tall = lane_iota((tall_rows, width))
@@ -107,7 +96,9 @@
     ):
         for p in range(fields // 2):
             tall[:height] = cols_ref[c_near, p]
-            tall[height:] = near[slot][p]
+            tall[height:] = jnp.zeros((8, width), jnp.float32)
+            tall[height : height + 1] = north[height + slot, p : p + 1]
+            tall[height + 7 :] = south[height + slot, p : p + 1]
             value = tall[...]
             tall[:height] = cols_ref[c_far, p]
             tall[height:] = jnp.zeros((8, width), jnp.float32)
@@ -121,7 +112,9 @@
         out_ref[2 * (fields // 2) * tall_rows :] = grid_ref[...]
 
 
-def tendency_kernel(state_ref, halo_ref, wide_ref, own_w_ref, own_e_ref, got_w_ref, got_e_ref, out_ref, faces, edge_lap, *, levels):
+def tendency_kernel(
+    state_ref, below_ref, above_ref, wide_ref, own_w_ref, own_e_ref, got_w_ref, got_e_ref, out_ref, faces, edge_lap, halo, *, levels
+):
     step = pl.program_id(0)
     fields, block, height, width = state_ref.shape
     rows = height + 8
@@ -141,6 +134,7 @@
 
     @pl.when(step == 0)
     def _():
+        halo[...] = jnp.zeros(halo.shape, jnp.float32)
         wide = wide_ref[...]
         east = jnp.where(last, pltpu.roll(part(got_e_ref, False, 0), width - 1 - levels, 1), pltpu.roll(wide, width - 1, 1))
         west = jnp.where(first, pltpu.roll(part(got_w_ref, False, 0), width - levels, 1), pltpu.roll(wide, 1, 1))
@@ -163,13 +157,17 @@
     wide = wide_ref[...]
     low = slice(0, height)
     for kk in range(block):
+        for f in range(fields):
+            halo[f, kk, 0:2] = above_ref[f, kk]
+            halo[f, kk, 6:8] = below_ref[f, kk]
+    for kk in range(block):
         level = step * block + kk
         depth = level.astype(jnp.float32)
         on_e, on_w, on_n, on_s = (depth < faces[n] for n in range(4))
         here_on = depth < wide[low]
         around = []
         for f in range(fields):
-            x = jnp.concatenate([state_ref[f, kk], halo_ref[f, kk]], axis=0)
+            x = jnp.concatenate([state_ref[f, kk], halo[f, kk]], axis=0)
             spot = (f % 2) * HALF + level
             p = f // 2
             east = jnp.where(last, pltpu.roll(part(got_e_ref, False, p), width - 1 - spot, 1), pltpu.roll(x, width - 1, 1))
@@ -296,15 +294,19 @@
     pairs = fields // 2
     rows = height + 8
     whole = lambda shape: pl.BlockSpec(shape, lambda i: (0,) * len(shape))
-    message = (fields * levels + height, 2, width)
-    north_msg, south_msg, pair, cols = pl.pallas_call(
+    small = (height + 2, 2, width)
+    edge_rows = pl.BlockSpec((fields, block, 2, width), lambda i: (0, i, 0, 0))
+    row_shape = jax.ShapeDtypeStruct((fields, levels, 2, width), f32)
+    up_rows, down_rows, north_msg, south_msg, pair, cols = pl.pallas_call(
         functools.partial(pack_kernel, levels=levels),
         grid=(levels // block,),
         in_specs=[whole((height, width))] * 3 + [pl.BlockSpec((fields, block, height, width), lambda i: (0, i, 0, 0))],
-        out_specs=[whole(message), whole(message), whole((height, 2, width)), whole((4, pairs, height, width))],
+        out_specs=[edge_rows, edge_rows, whole(small), whole(small), whole((height, 2, width)), whole((4, pairs, height, width))],
         out_shape=[
-            jax.ShapeDtypeStruct(message, f32),
-            jax.ShapeDtypeStruct(message, f32),
+            row_shape,
+            row_shape,
+            jax.ShapeDtypeStruct(small, f32),
+            jax.ShapeDtypeStruct(small, f32),
             jax.ShapeDtypeStruct((height, 2, width), f32),
             jax.ShapeDtypeStruct((4, pairs, height, width), f32),
         ],
@@ -315,16 +317,17 @@
     from_lat = [
         shifted(south_msg if b == 1 else north_msg if b == lats - 1 else pair, "lat", b) for b in range(1, lats)
     ]
+    above = shifted(down_rows, "lat", 1)
+    below = shifted(up_rows, "lat", lats - 1)
     smem = pl.BlockSpec(memory_space=pltpu.SMEM)
     vmem = pl.BlockSpec(memory_space=pltpu.VMEM)
     strip = 2 * pairs * rows
     cells = lats * 2 * height
-    halo, wide, west_msg, east_msg, grid = pl.pallas_call(
+    wide, west_msg, east_msg, grid = pl.pallas_call(
         functools.partial(middle_kernel, levels=levels, fields=fields, lats=lats),
         in_specs=[smem] + [vmem] * (2 + lats - 1),
-        out_specs=[vmem] * 5,
+        out_specs=[vmem] * 4,
         out_shape=[
-            jax.ShapeDtypeStruct((fields, levels, 8, width), f32),
             jax.ShapeDtypeStruct((rows, width), f32),
             jax.ShapeDtypeStruct((strip + cells, width), f32),
             jax.ShapeDtypeStruct((strip + cells, width), f32),
@@ -341,16 +344,17 @@
         grid=(levels // block,),
         in_specs=[
             pl.BlockSpec((fields, block, height, width), lambda i: (0, i, 0, 0)),
-            pl.BlockSpec((fields, block, 8, width), lambda i: (0, i, 0, 0)),
+            edge_rows,
+            edge_rows,
             whole((rows, width)),
         ]
         + [whole((strip, width))] * 4,
         out_specs=pl.BlockSpec((fields, block, height, width), lambda i: (0, i, 0, 0)),
         out_shape=jax.ShapeDtypeStruct(state.shape, f32),
-        scratch_shapes=[pltpu.VMEM((4, rows, width), f32), pltpu.VMEM((2, pairs, rows, width), f32)],
+        scratch_shapes=[pltpu.VMEM((4, rows, width), f32), pltpu.VMEM((2, pairs, rows, width), f32), pltpu.VMEM((fields, block, 8, width), f32)],
         cost_estimate=pl.CostEstimate(flops=100 * state.size, bytes_accessed=9 * state.size, transcendentals=0),
         name="tendency",
-    )(state, halo, wide, west_msg, east_msg, got[lons - 1], got[1])
+    )(state, below, above, wide, west_msg, east_msg, got[lons - 1], got[1])
 
     field = pltpu.VMEM((lats * height, lons * width), f32)
     surface, residual = pl.pallas_call(

time: 48 us -> 46 us (0.958)
  waiting for transfers between devices: 11.4 us -> 3.36 us
  starting transfers between devices: 12.3 us -> 19.1 us
  Pallas kernels: 21.2 us -> 20.6 us
    ppermute x10 -> x12, waiting for transfers between devices: 11.4 us -> 3.36 us  [shifted(): lax.ppermute(x, axis, [((i + distance) % count, i) for i in range(count)])]
    ppermute x10 -> x12, starting transfers between devices: 12.3 us -> 19.1 us  [shifted(): lax.ppermute(x, axis, [((i + distance) % count, i) for i in range(count)])]
    pallas_call x1, Pallas kernels: 2.54 us -> 1.75 us  [per_device(): pl.pallas_call(functools.partial(middle_kernel, levels=levels, fields=fie...]
    unnamed x20 -> x24, local copies, waits for them, and re-layouts: 2.16 us -> 1.96 us
  transfers between devices with their start and end apart: 10 -> 12, of which waited for: 4 -> 1; matrix products, arithmetic and copies ran while one was open for 0% -> 0% of each run, Pallas kernels for 18% -> 22%
where the time goes in v2:
time: 46 us; the launch traced here: 45.8 us
  Pallas kernels  20.6 us (45%)
  starting transfers between devices  19.1 us (42%)
  waiting for transfers between devices  3.36 us (7%)
  local copies, waits for them, and re-layouts  1.96 us (4%)
  between operations  0.73 us (2%)
    ppermute x12, starting transfers between devices, shifted(): lax.ppermute(x, axis, [((i + distance) % count, i) for i in range(count)])  19.1 us
    pallas_call x1, Pallas kernels, per_device(): pl.pallas_call(functools.partial(tendency_kernel, levels=levels), grid=(l...  8.55 us
    pallas_call x1, Pallas kernels, per_device(): pl.pallas_call(functools.partial(pack_kernel, levels=levels), grid=(level...  5.29 us
    pallas_call x1, Pallas kernels, per_device(): pl.pallas_call(functools.partial(solve_kernel, levels=levels, lats=lats,...  5.02 us
    ppermute x12, waiting for transfers between devices, shifted(): lax.ppermute(x, axis, [((i + distance) % count, i) for i in range(count)])  3.36 us
    unnamed x24, local copies, waits for them, and re-layouts  1.96 us
    pallas_call x1, Pallas kernels, per_device(): pl.pallas_call(functools.partial(middle_kernel, levels=levels, fields=fie...  1.75 us
  transfers between devices with their start and end apart: 12, of which 1 were waited for; matrix products, arithmetic and copies ran while one was open for 0% of the time, Pallas kernels for 22%

profile of v2, /device:TPU:0, one launch (start us, length us, event | category | flops | bytes accessed | tf_op | source)
XLA Modules:
  0.0 45.8 jit_solution(15733211035413402258)
XLA Ops:
  0.6 5.3 %pack.1 = (f32[4,40,2,128]{3,2,1,0:T(2,128)}, f32[4,40,2,128]{3,2,1,0:T(2,128)}, f32[26,2,128]{2,1,0:T(2,128)}, f32[26,2,128]{2,1,0:T(2,128)}, f32[24,2,128]{2,1,0:T(2,128)}, /*index=5*/f32[4,2,24,128]{3,2,1,0:T(8,128)}) custom-call(f32[24,128]{1,0:T(8,128)} %force_ref.1, s32[24,128]{1,0:T(8,128)} %sea_ref.1, s32[24,128]{1,0:T(8,128)} %count_ref.1, ...), custom_call_target="tpu_custom_call" | custom-call | tf_op jit(solution)/shard_map/pack/pallas_call | solution.py:300
  5.9 5.1 %collective-permute-start = (f32[26,2,128]{2,1,0:T(2,128)}, f32[26,2,128]{2,1,0:T(2,128)S(1)}, u32[]{:S(2)}, u32[]{:S(2)}) collective-permute-start(f32[26,2,128]{2,1,0:T(2,128)} %get-tuple-element.17), channel_id=1, source_target_pairs={{1,0},{2,1},{3,2},{0,3},{5,4},{6,5},{7,6},{4,7},{9,8},{10,9},{11,1... | collective-permute-start | bytes 79880 | tf_op jit(solution)/shard_map/ppermute | solution.py:286
  11.1 0.0 collective-permute-start.2
  11.1 1.0 %collective-permute-start.1 = (f32[24,2,128]{2,1,0:T(2,128)}, f32[24,2,128]{2,1,0:T(2,128)S(1)}, u32[]{:S(2)}, u32[]{:S(2)}) collective-permute-start(f32[24,2,128]{2,1,0:T(2,128)} %get-tuple-element.16.refs_2_), channel_id=1, source_target_pairs={{2,0},{3,1},{0,2},{1,3},{6,4},{7,5},{4,6},{5,7},{10,8},{11,9},{8,1... | collective-permute-start | bytes 73736 | tf_op jit(solution)/shard_map/ppermute | solution.py:286
  12.1 3.4 %collective-permute-start.10 = (f32[4,40,2,128]{3,2,1,0:T(2,128)}, f32[4,40,2,128]{3,2,1,0:T(2,128)S(1)}, u32[]{:S(2)}, u32[]{:S(2)}) collective-permute-start(f32[4,40,2,128]{3,2,1,0:T(2,128)} %get-tuple-element.24), channel_id=1, source_target_pairs={{3,0},{0,1},{1,2},{2,3},{7,4},{4,5},{5,6},{6,7},{11,8},{8,9},{9,10... | collective-permute-start | bytes 491528 | tf_op jit(solution)/shard_map/ppermute | solution.py:286
  15.4 0.4 collective-permute-start.11
  15.9 3.3 %collective-permute-done.1.refs_4_ = f32[24,2,128]{2,1,0:T(2,128)S(1)} collective-permute-done((f32[24,2,128]{2,1,0:T(2,128)}, f32[24,2,128]{2,1,0:T(2,128)S(1)}, u32[]{:S(2)}, u32[]{:S(2)}) %collective-permute-start.1) | collective-permute-done | bytes 24608 | tf_op jit(solution)/shard_map/ppermute | solution.py:286
  19.2 0.0 collective-permute-done.refs_3_
  19.2 0.0 collective-permute-done.2.refs_5_
  19.3 0.6 %copy-done.11 = f32[24,2,128]{2,1,0:T(2,128)} copy-done((f32[24,2,128]{2,1,0:T(2,128)}, f32[24,2,128]{2,1,0:T(2,128)S(1)}, u32[]{:S(2)}) %copy-start.11) | copy-done | bytes 24600
  19.8 0.0 copy-done.9
  19.8 0.0 copy-done.10
  19.9 1.8 %middle.1 = (f32[32,128]{1,0:T(8,128)}, f32[320,128]{1,0:T(8,128)}, f32[320,128]{1,0:T(8,128)}, f32[192,128]{1,0:T(8,128)}) custom-call(s32[1]{0:T(128)} %bitcast.refs_0_, f32[4,2,24,128]{3,2,1,0:T(8,128)} %get-tuple-element.15.refs_1_, f32[24,2,128]{2,1,0:T(2,128)} %get-tuple-element.16.refs_2_, f32[26,2,128]{2,1,0:T(2,128)} %copy-done.9, ...), custom_call_target="tpu_custom_call" | custom-call | tf_op jit(solution)/shard_map/middle/pallas_call | solution.py:326
  21.6 0.0 collective-permute-start.3
  21.6 0.5 %collective-permute-start.9 = (f32[320,128]{1,0:T(8,128)}, f32[320,128]{1,0:T(8,128)S(1)}, u32[]{:S(2)}, u32[]{:S(2)}) collective-permute-start(f32[320,128]{1,0:T(8,128)} %get-tuple-element.21.own_e_ref), channel_id=1, source_target_pairs={{28,0},{0,4},{4,8},{8,12},{12,16},{16,20},{20,24},{24,28},{29,1},{... | collective-permute-start | bytes 491528 | tf_op jit(solution)/shard_map/ppermute | solution.py:286
  22.1 1.5 %collective-permute-start.8 = (f32[192,128]{1,0:T(8,128)}, f32[192,128]{1,0:T(8,128)S(1)}, u32[]{:S(2)}, u32[]{:S(2)}) collective-permute-start(f32[192,128]{1,0:T(8,128)} %get-tuple-element.19.refs_1_), channel_id=1, source_target_pairs={{24,0},{28,4},{0,8},{4,12},{8,16},{12,20},{16,24},{20,28},{25,1},{... | collective-permute-start | bytes 294920 | tf_op jit(solution)/shard_map/ppermute | solution.py:286
  23.6 0.0 collective-permute-done.10.below_ref
  23.6 1.9 %collective-permute-start.7 = (f32[192,128]{1,0:T(8,128)}, f32[192,128]{1,0:T(8,128)S(1)}, u32[]{:S(2)}, u32[]{:S(2)}) collective-permute-start(f32[192,128]{1,0:T(8,128)} %get-tuple-element.19.refs_1_), channel_id=1, source_target_pairs={{20,0},{24,4},{28,8},{0,12},{4,16},{8,20},{12,24},{16,28},{21,1},{... | collective-permute-start | bytes 294920 | tf_op jit(solution)/shard_map/ppermute | solution.py:286
  25.5 0.5 %collective-permute-start.6 = (f32[192,128]{1,0:T(8,128)}, f32[192,128]{1,0:T(8,128)S(1)}, u32[]{:S(2)}, u32[]{:S(2)}) collective-permute-start(f32[192,128]{1,0:T(8,128)} %get-tuple-element.19.refs_1_), channel_id=1, source_target_pairs={{16,0},{20,4},{24,8},{28,12},{0,16},{4,20},{8,24},{12,28},{17,1},{... | collective-permute-start | bytes 294920 | tf_op jit(solution)/shard_map/ppermute | solution.py:286
  26.1 0.0 collective-permute-done.3.refs_2_.got_e_ref
  26.1 3.6 %collective-permute-start.5 = (f32[192,128]{1,0:T(8,128)}, f32[192,128]{1,0:T(8,128)S(1)}, u32[]{:S(2)}, u32[]{:S(2)}) collective-permute-start(f32[192,128]{1,0:T(8,128)} %get-tuple-element.19.refs_1_), channel_id=1, source_target_pairs={{12,0},{16,4},{20,8},{24,12},{28,16},{0,20},{4,24},{8,28},{13,1},{... | collective-permute-start | bytes 294920 | tf_op jit(solution)/shard_map/ppermute | solution.py:286
  29.6 0.0 collective-permute-done.9.refs_8_.got_w_ref
  29.6 1.2 %collective-permute-start.4 = (f32[192,128]{1,0:T(8,128)}, f32[192,128]{1,0:T(8,128)S(1)}, u32[]{:S(2)}, u32[]{:S(2)}) collective-permute-start(f32[192,128]{1,0:T(8,128)} %get-tuple-element.19.refs_1_), channel_id=1, source_target_pairs={{8,0},{12,4},{16,8},{20,12},{24,16},{28,20},{0,24},{4,28},{9,1},{1... | collective-permute-start | bytes 294920 | tf_op jit(solution)/shard_map/ppermute | solution.py:286
  30.8 8.5 %tendency.1 = f32[4,40,24,128]{3,2,1,0:T(8,128)} custom-call(f32[4,40,24,128]{3,2,1,0:T(8,128)} %state_ref.3, f32[4,40,2,128]{3,2,1,0:T(2,128)} %copy-done.2, f32[4,40,2,128]{3,2,1,0:T(2,128)} %copy-done.3, f32[32,128]{1,0:T(8,128)} %get-tuple-element.26.wide_ref, f32[320,128]{1,0:T(8,128)} %get-tuple-element.20.own_w_ref, ...), custom_call_target="tpu_custom_call" | custom-call | flops 49152000 | bytes 4423680 | tf_op jit(solution)/shard_map/tendency/pallas_call | solution.py:342
  39.4 0.0 collective-permute-done.6.refs_5_
  39.4 0.0 collective-permute-done.5.refs_4_
  39.4 0.6 %copy-done.4 = f32[192,128]{1,0:T(8,128)} copy-done((f32[192,128]{1,0:T(8,128)}, f32[192,128]{1,0:T(8,128)S(1)}, u32[]{:S(2)}) %copy-start.4) | copy-done | bytes 98328
  40.0 0.0 copy-done.5
  40.0 0.0 copy-done.6
  40.1 0.0 copy-done.7
  40.1 0.6 %copy-done.8 = f32[192,128]{1,0:T(8,128)} copy-done((f32[192,128]{1,0:T(8,128)}, f32[192,128]{1,0:T(8,128)S(1)}, u32[]{:S(2)}) %copy-start.8) | copy-done | bytes 98328
  40.7 5.0 %solve.1 = (f32[24,128]{1,0:T(8,128)}, f32[24,128]{1,0:T(8,128)}) custom-call(s32[1]{0:T(128)} %bitcast.refs_0_, f32[192,128]{1,0:T(8,128)} %get-tuple-element.19.refs_1_, f32[320,128]{1,0:T(8,128)} %copy-done, f32[192,128]{1,0:T(8,128)} %copy-done.8, f32[192,128]{1,0:T(8,128)} %copy-done.7, f32[192,128]{1,0:T(8,128)} %copy-done.6, f32[192,128]{1,0:T(8,128)} %copy-done.5, ...), custom_call_target="tpu_custom_call" | custom-call | tf_op jit(solution)/shard_map/solve/pallas_call | solution.py:360
  (20 shorter events, 0.0 us)
Async XLA Ops:
  5.9 13.3 %collective-permute-start = (f32[26,2,128]{2,1,0:T(2,128)}, f32[26,2,128]{2,1,0:T(2,128)S(1)}, u32[]{:S(2)}, u32[]{:S(2)}) collective-permute-start(f32[26,2,128]{2,1,0:T(2,128)} %get-tuple-element.17), channel_id=1, source_target_pairs={{1,0},{2,1},{3,2},{0,3},{5,4},{6,5},{7,6},{4,7},{9,8},{10,9},{11,1... | collective-permute-start | bytes 79880 | tf_op jit(solution)/shard_map/ppermute | solution.py:286
  11.1 8.2 %collective-permute-start.2 = (f32[26,2,128]{2,1,0:T(2,128)}, f32[26,2,128]{2,1,0:T(2,128)S(1)}, u32[]{:S(2)}, u32[]{:S(2)}) collective-permute-start(f32[26,2,128]{2,1,0:T(2,128)} %get-tuple-element.18), channel_id=1, source_target_pairs={{3,0},{0,1},{1,2},{2,3},{7,4},{4,5},{5,6},{6,7},{11,8},{8,9},{9,10... | collective-permute-start | bytes 79880 | tf_op jit(solution)/shard_map/ppermute | solution.py:286
  11.1 8.2 %collective-permute-start.1 = (f32[24,2,128]{2,1,0:T(2,128)}, f32[24,2,128]{2,1,0:T(2,128)S(1)}, u32[]{:S(2)}, u32[]{:S(2)}) collective-permute-start(f32[24,2,128]{2,1,0:T(2,128)} %get-tuple-element.16.refs_2_), channel_id=1, source_target_pairs={{2,0},{3,1},{0,2},{1,3},{6,4},{7,5},{4,6},{5,7},{10,8},{11,9},{8,1... | collective-permute-start | bytes 73736 | tf_op jit(solution)/shard_map/ppermute | solution.py:286
  12.1 11.6 %collective-permute-start.10 = (f32[4,40,2,128]{3,2,1,0:T(2,128)}, f32[4,40,2,128]{3,2,1,0:T(2,128)S(1)}, u32[]{:S(2)}, u32[]{:S(2)}) collective-permute-start(f32[4,40,2,128]{3,2,1,0:T(2,128)} %get-tuple-element.24), channel_id=1, source_target_pairs={{3,0},{0,1},{1,2},{2,3},{7,4},{4,5},{5,6},{6,7},{11,8},{8,9},{9,10... | collective-permute-start | bytes 491528 | tf_op jit(solution)/shard_map/ppermute | solution.py:286
  15.4 10.1 %collective-permute-start.11 = (f32[4,40,2,128]{3,2,1,0:T(2,128)}, f32[4,40,2,128]{3,2,1,0:T(2,128)S(1)}, u32[]{:S(2)}, u32[]{:S(2)}) collective-permute-start(f32[4,40,2,128]{3,2,1,0:T(2,128)} %get-tuple-element.25), channel_id=1, source_target_pairs={{1,0},{2,1},{3,2},{0,3},{5,4},{6,5},{7,6},{4,7},{9,8},{10,9},{11,1... | collective-permute-start | bytes 491528 | tf_op jit(solution)/shard_map/ppermute | solution.py:286
  19.2 0.6 %copy-start.11 = (f32[24,2,128]{2,1,0:T(2,128)}, f32[24,2,128]{2,1,0:T(2,128)S(1)}, u32[]{:S(2)}) copy-start(f32[24,2,128]{2,1,0:T(2,128)S(1)} %collective-permute-done.1.refs_4_) | copy-start | bytes 73732
  19.2 0.6 %copy-start.9 = (f32[26,2,128]{2,1,0:T(2,128)}, f32[26,2,128]{2,1,0:T(2,128)S(1)}, u32[]{:S(2)}) copy-start(f32[26,2,128]{2,1,0:T(2,128)S(1)} %collective-permute-done.refs_3_) | copy-start | bytes 79876
  19.2 0.6 %copy-start.10 = (f32[26,2,128]{2,1,0:T(2,128)}, f32[26,2,128]{2,1,0:T(2,128)S(1)}, u32[]{:S(2)}) copy-start(f32[26,2,128]{2,1,0:T(2,128)S(1)} %collective-permute-done.2.refs_5_) | copy-start | bytes 79876
  21.6 4.4 %collective-permute-start.3 = (f32[320,128]{1,0:T(8,128)}, f32[320,128]{1,0:T(8,128)S(1)}, u32[]{:S(2)}, u32[]{:S(2)}) collective-permute-start(f32[320,128]{1,0:T(8,128)} %get-tuple-element.20.own_w_ref), channel_id=1, source_target_pairs={{4,0},{8,4},{12,8},{16,12},{20,16},{24,20},{28,24},{0,28},{5,1},{9... | collective-permute-start | bytes 491528 | tf_op jit(solution)/shard_map/ppermute | solution.py:286
  21.6 8.0 %collective-permute-start.9 = (f32[320,128]{1,0:T(8,128)}, f32[320,128]{1,0:T(8,128)S(1)}, u32[]{:S(2)}, u32[]{:S(2)}) collective-permute-start(f32[320,128]{1,0:T(8,128)} %get-tuple-element.21.own_e_ref), channel_id=1, source_target_pairs={{28,0},{0,4},{4,8},{8,12},{12,16},{16,20},{20,24},{24,28},{29,1},{... | collective-permute-start | bytes 491528 | tf_op jit(solution)/shard_map/ppermute | solution.py:286
  22.1 17.2 %collective-permute-start.8 = (f32[192,128]{1,0:T(8,128)}, f32[192,128]{1,0:T(8,128)S(1)}, u32[]{:S(2)}, u32[]{:S(2)}) collective-permute-start(f32[192,128]{1,0:T(8,128)} %get-tuple-element.19.refs_1_), channel_id=1, source_target_pairs={{24,0},{28,4},{0,8},{4,12},{8,16},{12,20},{16,24},{20,28},{25,1},{... | collective-permute-start | bytes 294920 | tf_op jit(solution)/shard_map/ppermute | solution.py:286
  23.6 7.2 %copy-start.2 = (f32[4,40,2,128]{3,2,1,0:T(2,128)}, f32[4,40,2,128]{3,2,1,0:T(2,128)S(1)}, u32[]{:S(2)}) copy-start(f32[4,40,2,128]{3,2,1,0:T(2,128)S(1)} %collective-permute-done.10.below_ref) | copy-start | bytes 491524
  23.6 15.7 %collective-permute-start.7 = (f32[192,128]{1,0:T(8,128)}, f32[192,128]{1,0:T(8,128)S(1)}, u32[]{:S(2)}, u32[]{:S(2)}) collective-permute-start(f32[192,128]{1,0:T(8,128)} %get-tuple-element.19.refs_1_), channel_id=1, source_target_pairs={{20,0},{24,4},{28,8},{0,12},{4,16},{8,20},{12,24},{16,28},{21,1},{... | collective-permute-start | bytes 294920 | tf_op jit(solution)/shard_map/ppermute | solution.py:286
  25.5 5.2 %copy-start.3 = (f32[4,40,2,128]{3,2,1,0:T(2,128)}, f32[4,40,2,128]{3,2,1,0:T(2,128)S(1)}, u32[]{:S(2)}) copy-start(f32[4,40,2,128]{3,2,1,0:T(2,128)S(1)} %collective-permute-done.11.above_ref) | copy-start | bytes 491524
  25.5 13.8 %collective-permute-start.6 = (f32[192,128]{1,0:T(8,128)}, f32[192,128]{1,0:T(8,128)S(1)}, u32[]{:S(2)}, u32[]{:S(2)}) collective-permute-start(f32[192,128]{1,0:T(8,128)} %get-tuple-element.19.refs_1_), channel_id=1, source_target_pairs={{16,0},{20,4},{24,8},{28,12},{0,16},{4,20},{8,24},{12,28},{17,1},{... | collective-permute-start | bytes 294920 | tf_op jit(solution)/shard_map/ppermute | solution.py:286
  26.1 4.7 %copy-start = (f32[320,128]{1,0:T(8,128)}, f32[320,128]{1,0:T(8,128)S(1)}, u32[]{:S(2)}) copy-start(f32[320,128]{1,0:T(8,128)S(1)} %collective-permute-done.3.refs_2_.got_e_ref) | copy-start | bytes 491524
  26.1 13.3 %collective-permute-start.5 = (f32[192,128]{1,0:T(8,128)}, f32[192,128]{1,0:T(8,128)S(1)}, u32[]{:S(2)}, u32[]{:S(2)}) collective-permute-start(f32[192,128]{1,0:T(8,128)} %get-tuple-element.19.refs_1_), channel_id=1, source_target_pairs={{12,0},{16,4},{20,8},{24,12},{28,16},{0,20},{4,24},{8,28},{13,1},{... | collective-permute-start | bytes 294920 | tf_op jit(solution)/shard_map/ppermute | solution.py:286
  29.6 1.2 %copy-start.1 = (f32[320,128]{1,0:T(8,128)}, f32[320,128]{1,0:T(8,128)S(1)}, u32[]{:S(2)}) copy-start(f32[320,128]{1,0:T(8,128)S(1)} %collective-permute-done.9.refs_8_.got_w_ref) | copy-start | bytes 491524
  29.6 9.8 %collective-permute-start.4 = (f32[192,128]{1,0:T(8,128)}, f32[192,128]{1,0:T(8,128)S(1)}, u32[]{:S(2)}, u32[]{:S(2)}) collective-permute-start(f32[192,128]{1,0:T(8,128)} %get-tuple-element.19.refs_1_), channel_id=1, source_target_pairs={{8,0},{12,4},{16,8},{20,12},{24,16},{28,20},{0,24},{4,28},{9,1},{1... | collective-permute-start | bytes 294920 | tf_op jit(solution)/shard_map/ppermute | solution.py:286
  39.3 0.6 %copy-start.4 = (f32[192,128]{1,0:T(8,128)}, f32[192,128]{1,0:T(8,128)S(1)}, u32[]{:S(2)}) copy-start(f32[192,128]{1,0:T(8,128)S(1)} %collective-permute-done.8.refs_7_) | copy-start | bytes 294916
  39.4 0.7 %copy-start.5 = (f32[192,128]{1,0:T(8,128)}, f32[192,128]{1,0:T(8,128)S(1)}, u32[]{:S(2)}) copy-start(f32[192,128]{1,0:T(8,128)S(1)} %collective-permute-done.7.refs_6_) | copy-start | bytes 294916
  39.4 0.7 %copy-start.6 = (f32[192,128]{1,0:T(8,128)}, f32[192,128]{1,0:T(8,128)S(1)}, u32[]{:S(2)}) copy-start(f32[192,128]{1,0:T(8,128)S(1)} %collective-permute-done.6.refs_5_) | copy-start | bytes 294916
  39.4 0.7 %copy-start.7 = (f32[192,128]{1,0:T(8,128)}, f32[192,128]{1,0:T(8,128)S(1)}, u32[]{:S(2)}) copy-start(f32[192,128]{1,0:T(8,128)S(1)} %collective-permute-done.5.refs_4_) | copy-start | bytes 294916
  40.1 0.6 %copy-start.8 = (f32[192,128]{1,0:T(8,128)}, f32[192,128]{1,0:T(8,128)S(1)}, u32[]{:S(2)}) copy-start(f32[192,128]{1,0:T(8,128)S(1)} %collective-permute-done.4.refs_3_) | copy-start | bytes 294916

commit v3 on v2

--- a/solution.py
+++ b/solution.py
@@ -22,23 +22,39 @@
     return LEVEL_BLOCK if levels % LEVEL_BLOCK == 0 else 1
 
 
-def pack_kernel(
-    force_ref, sea_ref, count_ref, state_ref, up_ref, down_ref, north_ref, south_ref, pair_ref, cols_ref, *, levels
-):
+def first_kernel(force_ref, sea_ref, count_ref, low_ref, high_ref, north_ref, south_ref, pair_ref):
+    fields, levels, band, width = low_ref.shape
+    height = force_ref.shape[0]
+    sea = sea_ref[...].astype(jnp.float32)
+    wet = sea * count_ref[...].astype(jnp.float32)
+    forcing = sea * force_ref[...]
+    half = height // 2
+    for n in range(half):
+        rows = slice(2 * n, 2 * n + 2)
+        for ref in (north_ref, south_ref, pair_ref):
+            ref[n] = forcing[rows]
+            ref[half + n] = wet[rows]
+    lane = lane_iota((band, width))
+    for state_ref, out_ref, row in ((high_ref, north_ref, band - 1), (low_ref, south_ref, 0)):
+        held = [[jnp.zeros((band, width), jnp.float32) for _ in range(fields // 2)] for _ in range(2)]
+        for f in range(fields):
+            for k in range(levels):
+                x = state_ref[f, k]
+                spot = (f % 2) * HALF + k
+                for slot, edge in enumerate((0, width - 1)):
+                    moved = pltpu.roll(x, (spot - edge) % width, 1)
+                    held[slot][f // 2] = jnp.where(lane == spot, moved, held[slot][f // 2])
+        for slot in range(2):
+            for p in range(fields // 2):
+                out_ref[height + slot, p : p + 1] = held[slot][p][row : row + 1]
+
+
+def pack_kernel(state_ref, up_ref, down_ref, cols_ref):
     step = pl.program_id(0)
     fields, block, height, width = state_ref.shape
 
     @pl.when(step == 0)
     def _():
-        sea = sea_ref[...].astype(jnp.float32)
-        wet = sea * count_ref[...].astype(jnp.float32)
-        forcing = sea * force_ref[...]
-        half = height // 2
-        for n in range(half):
-            rows = slice(2 * n, 2 * n + 2)
-            for ref in (north_ref, south_ref, pair_ref):
-                ref[n] = forcing[rows]
-                ref[half + n] = wet[rows]
         cols_ref[...] = jnp.zeros(cols_ref.shape, jnp.float32)
 
     lane = lane_iota((height, width))
@@ -58,10 +74,6 @@
     for c in range(4):
         for p in range(fields // 2):
             cols_ref[c, p] = held[c][p]
-    for slot, c in enumerate((0, 3)):
-        for p in range(fields // 2):
-            north_ref[height + slot, p : p + 1] = held[c][p][height - 1 :]
-            south_ref[height + slot, p : p + 1] = held[c][p][:1]
 
 
 def middle_kernel(*refs, levels, fields, lats):
@@ -297,21 +309,33 @@
     small = (height + 2, 2, width)
     edge_rows = pl.BlockSpec((fields, block, 2, width), lambda i: (0, i, 0, 0))
     row_shape = jax.ShapeDtypeStruct((fields, levels, 2, width), f32)
-    up_rows, down_rows, north_msg, south_msg, pair, cols = pl.pallas_call(
-        functools.partial(pack_kernel, levels=levels),
-        grid=(levels // block,),
-        in_specs=[whole((height, width))] * 3 + [pl.BlockSpec((fields, block, height, width), lambda i: (0, i, 0, 0))],
-        out_specs=[edge_rows, edge_rows, whole(small), whole(small), whole((height, 2, width)), whole((4, pairs, height, width))],
+    band = 8
+    cells_block = whole((height, width))
+    north_msg, south_msg, pair = pl.pallas_call(
+        first_kernel,
+        grid=(1,),
+        in_specs=[cells_block] * 3
+        + [
+            pl.BlockSpec((fields, levels, band, width), lambda i: (0, 0, 0, 0)),
+            pl.BlockSpec((fields, levels, band, width), lambda i: (0, 0, height // band - 1, 0)),
+        ],
+        out_specs=[whole(small), whole(small), whole((height, 2, width))],
         out_shape=[
-            row_shape,
-            row_shape,
             jax.ShapeDtypeStruct(small, f32),
             jax.ShapeDtypeStruct(small, f32),
             jax.ShapeDtypeStruct((height, 2, width), f32),
-            jax.ShapeDtypeStruct((4, pairs, height, width), f32),
         ],
+        name="first",
+    )(surface_forcing, sea_mask, level_count, state, state)
+    up_rows, down_rows, cols = pl.pallas_call(
+        pack_kernel,
+        grid=(levels // block,),
+        in_specs=[pl.BlockSpec((fields, block, height, width), lambda i: (0, i, 0, 0))],
+        out_specs=[edge_rows, edge_rows, whole((4, pairs, height, width))],
+        out_shape=[row_shape, row_shape, jax.ShapeDtypeStruct((4, pairs, height, width), f32)],
+        cost_estimate=pl.CostEstimate(flops=100 * state.size, bytes_accessed=5 * state.size, transcendentals=0),
         name="pack",
-    )(surface_forcing, sea_mask, level_count, state)
+    )(state)
 
     place = lax.axis_index("lat").astype(jnp.int32)[None]
     from_lat = [

time: 46 us -> 45.3 us (0.985)
  Pallas kernels: 20.6 us -> 23.2 us
  starting transfers between devices: 19.1 us -> 17.3 us
  waiting for transfers between devices: 3.36 us -> 1.76 us
    pallas_call x1 -> x2, Pallas kernels: 5.29 us -> 7.93 us  [the longest x1 5.22 us: per_device(): pl.pallas_call(pack_kernel, grid=(levels // block,), in_specs=[pl.BlockSp...]
    ppermute x12, starting transfers between devices: 19.1 us -> 17.3 us  [shifted(): lax.ppermute(x, axis, [((i + distance) % count, i) for i in range(count)])]
    ppermute x12, waiting for transfers between devices: 3.36 us -> 1.76 us  [shifted(): lax.ppermute(x, axis, [((i + distance) % count, i) for i in range(count)])]
  transfers between devices with their start and end apart: 12 -> 12, of which waited for: 1 -> 3; matrix products, arithmetic and copies ran while one was open for 0% -> 0% of each run, Pallas kernels for 22% -> 34%
where the time goes in v3:
time: 45.3 us; the launch traced here: 45 us
  Pallas kernels  23.2 us (51%)
  starting transfers between devices  17.3 us (38%)
  local copies, waits for them, and re-layouts  1.94 us (4%)
  waiting for transfers between devices  1.76 us (4%)
  between operations  0.74 us (2%)
    ppermute x12, starting transfers between devices, shifted(): lax.ppermute(x, axis, [((i + distance) % count, i) for i in range(count)])  17.3 us
    pallas_call x1, Pallas kernels, per_device(): pl.pallas_call(functools.partial(tendency_kernel, levels=levels), grid=(l...  8.55 us
    pallas_call x1, Pallas kernels, per_device(): pl.pallas_call(pack_kernel, grid=(levels // block,), in_specs=[pl.BlockSp...  5.22 us
    pallas_call x1, Pallas kernels, per_device(): pl.pallas_call(functools.partial(solve_kernel, levels=levels, lats=lats,...  5.02 us
    pallas_call x1, Pallas kernels, per_device(): pl.pallas_call(first_kernel, grid=(1,), in_specs=[cells_block] * 3 + [pl....  2.71 us
    unnamed x24, local copies, waits for them, and re-layouts  1.94 us
    ppermute x12, waiting for transfers between devices, shifted(): lax.ppermute(x, axis, [((i + distance) % count, i) for i in range(count)])  1.76 us
    pallas_call x1, Pallas kernels, per_device(): pl.pallas_call(functools.partial(middle_kernel, levels=levels, fields=fie...  1.75 us
  transfers between devices with their start and end apart: 12, of which 3 were waited for; matrix products, arithmetic and copies ran while one was open for 0% of the time, Pallas kernels for 34%

profile of v3, /device:TPU:0, one launch (start us, length us, event | category | flops | bytes accessed | tf_op | source)
XLA Modules:
  0.0 45.0 jit_solution(11652373614261752048)
XLA Ops:
  0.6 2.7 %first.1 = (f32[26,2,128]{2,1,0:T(2,128)}, f32[26,2,128]{2,1,0:T(2,128)}, f32[24,2,128]{2,1,0:T(2,128)}) custom-call(f32[24,128]{1,0:T(8,128)} %force_ref.1, s32[24,128]{1,0:T(8,128)} %sea_ref.1, s32[24,128]{1,0:T(8,128)} %count_ref.1, f32[4,40,24,128]{3,2,1,0:T(8,128)} %state_ref.3, f32[4,40,24,128]{3,2,1,0:T(8,128)} %state_ref.3), custom_call_target="tpu_custom_call" | custom-call | tf_op jit(solution)/shard_map/first/pallas_call | solution.py:314
  3.3 5.1 %collective-permute-start = (f32[26,2,128]{2,1,0:T(2,128)}, f32[26,2,128]{2,1,0:T(2,128)S(1)}, u32[]{:S(2)}, u32[]{:S(2)}) collective-permute-start(f32[26,2,128]{2,1,0:T(2,128)} %get-tuple-element.17), channel_id=1, source_target_pairs={{1,0},{2,1},{3,2},{0,3},{5,4},{6,5},{7,6},{4,7},{9,8},{10,9},{11,1... | collective-permute-start | bytes 79880 | tf_op jit(solution)/shard_map/ppermute | solution.py:298
  8.4 1.0 %collective-permute-start.1 = (f32[24,2,128]{2,1,0:T(2,128)}, f32[24,2,128]{2,1,0:T(2,128)S(1)}, u32[]{:S(2)}, u32[]{:S(2)}) collective-permute-start(f32[24,2,128]{2,1,0:T(2,128)} %get-tuple-element.16.refs_2_), channel_id=1, source_target_pairs={{2,0},{3,1},{0,2},{1,3},{6,4},{7,5},{4,6},{5,7},{10,8},{11,9},{8,1... | collective-permute-start | bytes 73736 | tf_op jit(solution)/shard_map/ppermute | solution.py:298
  9.4 5.2 %pack.1 = (f32[4,40,2,128]{3,2,1,0:T(2,128)}, f32[4,40,2,128]{3,2,1,0:T(2,128)}, f32[4,2,24,128]{3,2,1,0:T(8,128)}) custom-call(f32[4,40,24,128]{3,2,1,0:T(8,128)} %state_ref.3), custom_call_target="tpu_custom_call" | custom-call | flops 49152000 | bytes 2457600 | tf_op jit(solution)/shard_map/pack/pallas_call | solution.py:330
  14.6 3.4 %collective-permute-start.10 = (f32[4,40,2,128]{3,2,1,0:T(2,128)}, f32[4,40,2,128]{3,2,1,0:T(2,128)S(1)}, u32[]{:S(2)}, u32[]{:S(2)}) collective-permute-start(f32[4,40,2,128]{3,2,1,0:T(2,128)} %get-tuple-element.24), channel_id=1, source_target_pairs={{3,0},{0,1},{1,2},{2,3},{7,4},{4,5},{5,6},{6,7},{11,8},{8,9},{9,10... | collective-permute-start | bytes 491528 | tf_op jit(solution)/shard_map/ppermute | solution.py:298
  18.0 0.4 collective-permute-start.11
  18.5 0.0 collective-permute-done.1.refs_4_
  18.5 0.0 collective-permute-done.refs_3_
  18.5 0.0 collective-permute-done.2.refs_5_
  18.5 0.6 %copy-done.11 = f32[24,2,128]{2,1,0:T(2,128)} copy-done((f32[24,2,128]{2,1,0:T(2,128)}, f32[24,2,128]{2,1,0:T(2,128)S(1)}, u32[]{:S(2)}) %copy-start.11) | copy-done | bytes 24600
  19.1 0.0 copy-done.9
  19.1 0.0 copy-done.10
  19.1 1.7 %middle.1 = (f32[32,128]{1,0:T(8,128)}, f32[320,128]{1,0:T(8,128)}, f32[320,128]{1,0:T(8,128)}, f32[192,128]{1,0:T(8,128)}) custom-call(s32[1]{0:T(128)} %bitcast.refs_0_, f32[4,2,24,128]{3,2,1,0:T(8,128)} %get-tuple-element.15.refs_1_, f32[24,2,128]{2,1,0:T(2,128)} %get-tuple-element.16.refs_2_, f32[26,2,128]{2,1,0:T(2,128)} %copy-done.9, ...), custom_call_target="tpu_custom_call" | custom-call | tf_op jit(solution)/shard_map/middle/pallas_call | solution.py:350
  20.9 0.5 %collective-permute-start.3 = (f32[320,128]{1,0:T(8,128)}, f32[320,128]{1,0:T(8,128)S(1)}, u32[]{:S(2)}, u32[]{:S(2)}) collective-permute-start(f32[320,128]{1,0:T(8,128)} %get-tuple-element.20.own_w_ref), channel_id=1, source_target_pairs={{4,0},{8,4},{12,8},{16,12},{20,16},{24,20},{28,24},{0,28},{5,1},{9... | collective-permute-start | bytes 491528 | tf_op jit(solution)/shard_map/ppermute | solution.py:298
  21.4 0.0 collective-permute-start.9
  21.4 1.5 %collective-permute-start.8 = (f32[192,128]{1,0:T(8,128)}, f32[192,128]{1,0:T(8,128)S(1)}, u32[]{:S(2)}, u32[]{:S(2)}) collective-permute-start(f32[192,128]{1,0:T(8,128)} %get-tuple-element.19.refs_1_), channel_id=1, source_target_pairs={{24,0},{28,4},{0,8},{4,12},{8,16},{12,20},{16,24},{20,28},{25,1},{... | collective-permute-start | bytes 294920 | tf_op jit(solution)/shard_map/ppermute | solution.py:298
  22.9 0.7 %collective-permute-done.10.below_ref = f32[4,40,2,128]{3,2,1,0:T(2,128)S(1)} collective-permute-done((f32[4,40,2,128]{3,2,1,0:T(2,128)}, f32[4,40,2,128]{3,2,1,0:T(2,128)S(1)}, u32[]{:S(2)}, u32[]{:S(2)}) %collective-permute-start.10) | collective-permute-done | bytes 163872 | tf_op jit(solution)/shard_map/ppermute | solution.py:298
  23.5 1.3 %collective-permute-start.7 = (f32[192,128]{1,0:T(8,128)}, f32[192,128]{1,0:T(8,128)S(1)}, u32[]{:S(2)}, u32[]{:S(2)}) collective-permute-start(f32[192,128]{1,0:T(8,128)} %get-tuple-element.19.refs_1_), channel_id=1, source_target_pairs={{20,0},{24,4},{28,8},{0,12},{4,16},{8,20},{12,24},{16,28},{21,1},{... | collective-permute-start | bytes 294920 | tf_op jit(solution)/shard_map/ppermute | solution.py:298
  24.8 0.5 %collective-permute-done.11.above_ref = f32[4,40,2,128]{3,2,1,0:T(2,128)S(1)} collective-permute-done((f32[4,40,2,128]{3,2,1,0:T(2,128)}, f32[4,40,2,128]{3,2,1,0:T(2,128)S(1)}, u32[]{:S(2)}, u32[]{:S(2)}) %collective-permute-start.11) | collective-permute-done | bytes 163872 | tf_op jit(solution)/shard_map/ppermute | solution.py:298
  25.3 1.5 %collective-permute-start.6 = (f32[192,128]{1,0:T(8,128)}, f32[192,128]{1,0:T(8,128)S(1)}, u32[]{:S(2)}, u32[]{:S(2)}) collective-permute-start(f32[192,128]{1,0:T(8,128)} %get-tuple-element.19.refs_1_), channel_id=1, source_target_pairs={{16,0},{20,4},{24,8},{28,12},{0,16},{4,20},{8,24},{12,28},{17,1},{... | collective-permute-start | bytes 294920 | tf_op jit(solution)/shard_map/ppermute | solution.py:298
  26.8 0.0 collective-permute-done.3.refs_2_.got_e_ref
  26.8 1.7 %collective-permute-start.5 = (f32[192,128]{1,0:T(8,128)}, f32[192,128]{1,0:T(8,128)S(1)}, u32[]{:S(2)}, u32[]{:S(2)}) collective-permute-start(f32[192,128]{1,0:T(8,128)} %get-tuple-element.19.refs_1_), channel_id=1, source_target_pairs={{12,0},{16,4},{20,8},{24,12},{28,16},{0,20},{4,24},{8,28},{13,1},{... | collective-permute-start | bytes 294920 | tf_op jit(solution)/shard_map/ppermute | solution.py:298
  28.5 0.6 %collective-permute-done.9.refs_8_.got_w_ref = f32[320,128]{1,0:T(8,128)S(1)} collective-permute-done((f32[320,128]{1,0:T(8,128)}, f32[320,128]{1,0:T(8,128)S(1)}, u32[]{:S(2)}, u32[]{:S(2)}) %collective-permute-start.9) | collective-permute-done | bytes 163872 | tf_op jit(solution)/shard_map/ppermute | solution.py:298
  29.1 1.0 %collective-permute-start.4 = (f32[192,128]{1,0:T(8,128)}, f32[192,128]{1,0:T(8,128)S(1)}, u32[]{:S(2)}, u32[]{:S(2)}) collective-permute-start(f32[192,128]{1,0:T(8,128)} %get-tuple-element.19.refs_1_), channel_id=1, source_target_pairs={{8,0},{12,4},{16,8},{20,12},{24,16},{28,20},{0,24},{4,28},{9,1},{1... | collective-permute-start | bytes 294920 | tf_op jit(solution)/shard_map/ppermute | solution.py:298
  30.0 8.5 %tendency.1 = f32[4,40,24,128]{3,2,1,0:T(8,128)} custom-call(f32[4,40,24,128]{3,2,1,0:T(8,128)} %state_ref.3, f32[4,40,2,128]{3,2,1,0:T(2,128)} %copy-done.2, f32[4,40,2,128]{3,2,1,0:T(2,128)} %copy-done.3, f32[32,128]{1,0:T(8,128)} %get-tuple-element.26.wide_ref, f32[320,128]{1,0:T(8,128)} %get-tuple-element.20.own_w_ref, ...), custom_call_target="tpu_custom_call" | custom-call | flops 49152000 | bytes 4423680 | tf_op jit(solution)/shard_map/tendency/pallas_call | solution.py:366
  38.6 0.0 collective-permute-done.6.refs_5_
  38.7 0.6 %copy-done.4 = f32[192,128]{1,0:T(8,128)} copy-done((f32[192,128]{1,0:T(8,128)}, f32[192,128]{1,0:T(8,128)S(1)}, u32[]{:S(2)}) %copy-start.4) | copy-done | bytes 98328
  39.2 0.0 copy-done.5
  39.3 0.1 copy-done.6
  39.3 0.0 copy-done.7
  39.4 0.6 %copy-done.8 = f32[192,128]{1,0:T(8,128)} copy-done((f32[192,128]{1,0:T(8,128)}, f32[192,128]{1,0:T(8,128)S(1)}, u32[]{:S(2)}) %copy-start.8) | copy-done | bytes 98328
  40.0 5.0 %solve.1 = (f32[24,128]{1,0:T(8,128)}, f32[24,128]{1,0:T(8,128)}) custom-call(s32[1]{0:T(128)} %bitcast.refs_0_, f32[192,128]{1,0:T(8,128)} %get-tuple-element.19.refs_1_, f32[320,128]{1,0:T(8,128)} %copy-done, f32[192,128]{1,0:T(8,128)} %copy-done.8, f32[192,128]{1,0:T(8,128)} %copy-done.7, f32[192,128]{1,0:T(8,128)} %copy-done.6, f32[192,128]{1,0:T(8,128)} %copy-done.5, ...), custom_call_target="tpu_custom_call" | custom-call | tf_op jit(solution)/shard_map/solve/pallas_call | solution.py:384
  (21 shorter events, 0.0 us)
Async XLA Ops:
  3.3 15.1 %collective-permute-start = (f32[26,2,128]{2,1,0:T(2,128)}, f32[26,2,128]{2,1,0:T(2,128)S(1)}, u32[]{:S(2)}, u32[]{:S(2)}) collective-permute-start(f32[26,2,128]{2,1,0:T(2,128)} %get-tuple-element.17), channel_id=1, source_target_pairs={{1,0},{2,1},{3,2},{0,3},{5,4},{6,5},{7,6},{4,7},{9,8},{10,9},{11,1... | collective-permute-start | bytes 79880 | tf_op jit(solution)/shard_map/ppermute | solution.py:298
  8.4 10.1 %collective-permute-start.2 = (f32[26,2,128]{2,1,0:T(2,128)}, f32[26,2,128]{2,1,0:T(2,128)S(1)}, u32[]{:S(2)}, u32[]{:S(2)}) collective-permute-start(f32[26,2,128]{2,1,0:T(2,128)} %get-tuple-element.18), channel_id=1, source_target_pairs={{3,0},{0,1},{1,2},{2,3},{7,4},{4,5},{5,6},{6,7},{11,8},{8,9},{9,10... | collective-permute-start | bytes 79880 | tf_op jit(solution)/shard_map/ppermute | solution.py:298
  8.4 10.1 %collective-permute-start.1 = (f32[24,2,128]{2,1,0:T(2,128)}, f32[24,2,128]{2,1,0:T(2,128)S(1)}, u32[]{:S(2)}, u32[]{:S(2)}) collective-permute-start(f32[24,2,128]{2,1,0:T(2,128)} %get-tuple-element.16.refs_2_), channel_id=1, source_target_pairs={{2,0},{3,1},{0,2},{1,3},{6,4},{7,5},{4,6},{5,7},{10,8},{11,9},{8,1... | collective-permute-start | bytes 73736 | tf_op jit(solution)/shard_map/ppermute | solution.py:298
  14.6 8.9 %collective-permute-start.10 = (f32[4,40,2,128]{3,2,1,0:T(2,128)}, f32[4,40,2,128]{3,2,1,0:T(2,128)S(1)}, u32[]{:S(2)}, u32[]{:S(2)}) collective-permute-start(f32[4,40,2,128]{3,2,1,0:T(2,128)} %get-tuple-element.24), channel_id=1, source_target_pairs={{3,0},{0,1},{1,2},{2,3},{7,4},{4,5},{5,6},{6,7},{11,8},{8,9},{9,10... | collective-permute-start | bytes 491528 | tf_op jit(solution)/shard_map/ppermute | solution.py:298
  18.0 7.3 %collective-permute-start.11 = (f32[4,40,2,128]{3,2,1,0:T(2,128)}, f32[4,40,2,128]{3,2,1,0:T(2,128)S(1)}, u32[]{:S(2)}, u32[]{:S(2)}) collective-permute-start(f32[4,40,2,128]{3,2,1,0:T(2,128)} %get-tuple-element.25), channel_id=1, source_target_pairs={{1,0},{2,1},{3,2},{0,3},{5,4},{6,5},{7,6},{4,7},{9,8},{10,9},{11,1... | collective-permute-start | bytes 491528 | tf_op jit(solution)/shard_map/ppermute | solution.py:298
  18.5 0.6 %copy-start.11 = (f32[24,2,128]{2,1,0:T(2,128)}, f32[24,2,128]{2,1,0:T(2,128)S(1)}, u32[]{:S(2)}) copy-start(f32[24,2,128]{2,1,0:T(2,128)S(1)} %collective-permute-done.1.refs_4_) | copy-start | bytes 73732
  18.5 0.6 %copy-start.9 = (f32[26,2,128]{2,1,0:T(2,128)}, f32[26,2,128]{2,1,0:T(2,128)S(1)}, u32[]{:S(2)}) copy-start(f32[26,2,128]{2,1,0:T(2,128)S(1)} %collective-permute-done.refs_3_) | copy-start | bytes 79876
  18.5 0.6 %copy-start.10 = (f32[26,2,128]{2,1,0:T(2,128)}, f32[26,2,128]{2,1,0:T(2,128)S(1)}, u32[]{:S(2)}) copy-start(f32[26,2,128]{2,1,0:T(2,128)S(1)} %collective-permute-done.2.refs_5_) | copy-start | bytes 79876
  20.9 6.0 %collective-permute-start.3 = (f32[320,128]{1,0:T(8,128)}, f32[320,128]{1,0:T(8,128)S(1)}, u32[]{:S(2)}, u32[]{:S(2)}) collective-permute-start(f32[320,128]{1,0:T(8,128)} %get-tuple-element.20.own_w_ref), channel_id=1, source_target_pairs={{4,0},{8,4},{12,8},{16,12},{20,16},{24,20},{28,24},{0,28},{5,1},{9... | collective-permute-start | bytes 491528 | tf_op jit(solution)/shard_map/ppermute | solution.py:298
  21.4 7.7 %collective-permute-start.9 = (f32[320,128]{1,0:T(8,128)}, f32[320,128]{1,0:T(8,128)S(1)}, u32[]{:S(2)}, u32[]{:S(2)}) collective-permute-start(f32[320,128]{1,0:T(8,128)} %get-tuple-element.21.own_e_ref), channel_id=1, source_target_pairs={{28,0},{0,4},{4,8},{8,12},{12,16},{16,20},{20,24},{24,28},{29,1},{... | collective-permute-start | bytes 491528 | tf_op jit(solution)/shard_map/ppermute | solution.py:298
  21.4 17.2 %collective-permute-start.8 = (f32[192,128]{1,0:T(8,128)}, f32[192,128]{1,0:T(8,128)S(1)}, u32[]{:S(2)}, u32[]{:S(2)}) collective-permute-start(f32[192,128]{1,0:T(8,128)} %get-tuple-element.19.refs_1_), channel_id=1, source_target_pairs={{24,0},{28,4},{0,8},{4,12},{8,16},{12,20},{16,24},{20,28},{25,1},{... | collective-permute-start | bytes 294920 | tf_op jit(solution)/shard_map/ppermute | solution.py:298
  23.5 6.5 %copy-start.2 = (f32[4,40,2,128]{3,2,1,0:T(2,128)}, f32[4,40,2,128]{3,2,1,0:T(2,128)S(1)}, u32[]{:S(2)}) copy-start(f32[4,40,2,128]{3,2,1,0:T(2,128)S(1)} %collective-permute-done.10.below_ref) | copy-start | bytes 491524
  23.5 15.1 %collective-permute-start.7 = (f32[192,128]{1,0:T(8,128)}, f32[192,128]{1,0:T(8,128)S(1)}, u32[]{:S(2)}, u32[]{:S(2)}) collective-permute-start(f32[192,128]{1,0:T(8,128)} %get-tuple-element.19.refs_1_), channel_id=1, source_target_pairs={{20,0},{24,4},{28,8},{0,12},{4,16},{8,20},{12,24},{16,28},{21,1},{... | collective-permute-start | bytes 294920 | tf_op jit(solution)/shard_map/ppermute | solution.py:298
  25.3 4.7 %copy-start.3 = (f32[4,40,2,128]{3,2,1,0:T(2,128)}, f32[4,40,2,128]{3,2,1,0:T(2,128)S(1)}, u32[]{:S(2)}) copy-start(f32[4,40,2,128]{3,2,1,0:T(2,128)S(1)} %collective-permute-done.11.above_ref) | copy-start | bytes 491524
  25.3 13.3 %collective-permute-start.6 = (f32[192,128]{1,0:T(8,128)}, f32[192,128]{1,0:T(8,128)S(1)}, u32[]{:S(2)}, u32[]{:S(2)}) collective-permute-start(f32[192,128]{1,0:T(8,128)} %get-tuple-element.19.refs_1_), channel_id=1, source_target_pairs={{16,0},{20,4},{24,8},{28,12},{0,16},{4,20},{8,24},{12,28},{17,1},{... | collective-permute-start | bytes 294920 | tf_op jit(solution)/shard_map/ppermute | solution.py:298
  26.8 3.2 %copy-start = (f32[320,128]{1,0:T(8,128)}, f32[320,128]{1,0:T(8,128)S(1)}, u32[]{:S(2)}) copy-start(f32[320,128]{1,0:T(8,128)S(1)} %collective-permute-done.3.refs_2_.got_e_ref) | copy-start | bytes 491524
  26.8 11.8 %collective-permute-start.5 = (f32[192,128]{1,0:T(8,128)}, f32[192,128]{1,0:T(8,128)S(1)}, u32[]{:S(2)}, u32[]{:S(2)}) collective-permute-start(f32[192,128]{1,0:T(8,128)} %get-tuple-element.19.refs_1_), channel_id=1, source_target_pairs={{12,0},{16,4},{20,8},{24,12},{28,16},{0,20},{4,24},{8,28},{13,1},{... | collective-permute-start | bytes 294920 | tf_op jit(solution)/shard_map/ppermute | solution.py:298
  29.1 1.0 %copy-start.1 = (f32[320,128]{1,0:T(8,128)}, f32[320,128]{1,0:T(8,128)S(1)}, u32[]{:S(2)}) copy-start(f32[320,128]{1,0:T(8,128)S(1)} %collective-permute-done.9.refs_8_.got_w_ref) | copy-start | bytes 491524
  29.1 9.6 %collective-permute-start.4 = (f32[192,128]{1,0:T(8,128)}, f32[192,128]{1,0:T(8,128)S(1)}, u32[]{:S(2)}, u32[]{:S(2)}) collective-permute-start(f32[192,128]{1,0:T(8,128)} %get-tuple-element.19.refs_1_), channel_id=1, source_target_pairs={{8,0},{12,4},{16,8},{20,12},{24,16},{28,20},{0,24},{4,28},{9,1},{1... | collective-permute-start | bytes 294920 | tf_op jit(solution)/shard_map/ppermute | solution.py:298
  38.6 0.6 %copy-start.4 = (f32[192,128]{1,0:T(8,128)}, f32[192,128]{1,0:T(8,128)S(1)}, u32[]{:S(2)}) copy-start(f32[192,128]{1,0:T(8,128)S(1)} %collective-permute-done.8.refs_7_) | copy-start | bytes 294916
  38.6 0.7 %copy-start.5 = (f32[192,128]{1,0:T(8,128)}, f32[192,128]{1,0:T(8,128)S(1)}, u32[]{:S(2)}) copy-start(f32[192,128]{1,0:T(8,128)S(1)} %collective-permute-done.7.refs_6_) | copy-start | bytes 294916
  38.6 0.7 %copy-start.6 = (f32[192,128]{1,0:T(8,128)}, f32[192,128]{1,0:T(8,128)S(1)}, u32[]{:S(2)}) copy-start(f32[192,128]{1,0:T(8,128)S(1)} %collective-permute-done.6.refs_5_) | copy-start | bytes 294916
  38.6 0.7 %copy-start.7 = (f32[192,128]{1,0:T(8,128)}, f32[192,128]{1,0:T(8,128)S(1)}, u32[]{:S(2)}) copy-start(f32[192,128]{1,0:T(8,128)S(1)} %collective-permute-done.5.refs_4_) | copy-start | bytes 294916
  39.4 0.6 %copy-start.8 = (f32[192,128]{1,0:T(8,128)}, f32[192,128]{1,0:T(8,128)S(1)}, u32[]{:S(2)}) copy-start(f32[192,128]{1,0:T(8,128)S(1)} %collective-permute-done.4.refs_3_) | copy-start | bytes 294916

commit v4 on v3

--- a/solution.py
+++ b/solution.py
@@ -10,7 +10,7 @@
 ITERS = 4
 damping = 0.05
 viscosity = 0.02
-LEVEL_BLOCK = 8
+LEVEL_BLOCK = 4
 HALF = 64
 
 

time: 45.3 us -> 49.5 us (1.093)
  Pallas kernels: 23.2 us -> 27.1 us
    pallas_call x1, Pallas kernels: 5.22 us -> 7.49 us  [per_device(): pl.pallas_call(pack_kernel, grid=(levels // block,), in_specs=[pl.BlockSp...]
    pallas_call x1, Pallas kernels: 8.55 us -> 10.2 us  [per_device(): pl.pallas_call(functools.partial(tendency_kernel, levels=levels), grid=(l...]
  transfers between devices with their start and end apart: 12 -> 12, of which waited for: 3 -> 3; matrix products, arithmetic and copies ran while one was open for 0% -> 0% of each run, Pallas kernels for 34% -> 40%
where the time goes in v4:
time: 49.5 us; the launch traced here: 48.9 us
  Pallas kernels  27.1 us (55%)
  starting transfers between devices  17.3 us (35%)
  local copies, waits for them, and re-layouts  1.94 us (4%)
  waiting for transfers between devices  1.76 us (4%)
  between operations  0.74 us (1%)
    ppermute x12, starting transfers between devices, shifted(): lax.ppermute(x, axis, [((i + distance) % count, i) for i in range(count)])  17.3 us
    pallas_call x1, Pallas kernels, per_device(): pl.pallas_call(functools.partial(tendency_kernel, levels=levels), grid=(l...  10.2 us
    pallas_call x1, Pallas kernels, per_device(): pl.pallas_call(pack_kernel, grid=(levels // block,), in_specs=[pl.BlockSp...  7.49 us
    pallas_call x1, Pallas kernels, per_device(): pl.pallas_call(functools.partial(solve_kernel, levels=levels, lats=lats,...  5.02 us
    pallas_call x1, Pallas kernels, per_device(): pl.pallas_call(first_kernel, grid=(1,), in_specs=[cells_block] * 3 + [pl....  2.71 us
    unnamed x24, local copies, waits for them, and re-layouts  1.94 us
    ppermute x12, waiting for transfers between devices, shifted(): lax.ppermute(x, axis, [((i + distance) % count, i) for i in range(count)])  1.76 us
    pallas_call x1, Pallas kernels, per_device(): pl.pallas_call(functools.partial(middle_kernel, levels=levels, fields=fie...  1.75 us
  transfers between devices with their start and end apart: 12, of which 3 were waited for; matrix products, arithmetic and copies ran while one was open for 0% of the time, Pallas kernels for 40%

profile of v4, /device:TPU:0, one launch (start us, length us, event | category | flops | bytes accessed | tf_op | source)
XLA Modules:
  0.0 48.9 jit_solution(594755439930185438)
XLA Ops:
  0.6 2.7 %first.1 = (f32[26,2,128]{2,1,0:T(2,128)}, f32[26,2,128]{2,1,0:T(2,128)}, f32[24,2,128]{2,1,0:T(2,128)}) custom-call(f32[24,128]{1,0:T(8,128)} %force_ref.1, s32[24,128]{1,0:T(8,128)} %sea_ref.1, s32[24,128]{1,0:T(8,128)} %count_ref.1, f32[4,40,24,128]{3,2,1,0:T(8,128)} %state_ref.3, f32[4,40,24,128]{3,2,1,0:T(8,128)} %state_ref.3), custom_call_target="tpu_custom_call" | custom-call | tf_op jit(solution)/shard_map/first/pallas_call | solution.py:314
  3.3 5.1 %collective-permute-start = (f32[26,2,128]{2,1,0:T(2,128)}, f32[26,2,128]{2,1,0:T(2,128)S(1)}, u32[]{:S(2)}, u32[]{:S(2)}) collective-permute-start(f32[26,2,128]{2,1,0:T(2,128)} %get-tuple-element.17), channel_id=1, source_target_pairs={{1,0},{2,1},{3,2},{0,3},{5,4},{6,5},{7,6},{4,7},{9,8},{10,9},{11,1... | collective-permute-start | bytes 79880 | tf_op jit(solution)/shard_map/ppermute | solution.py:298
  8.4 0.0 collective-permute-start.2
  8.4 1.0 %collective-permute-start.1 = (f32[24,2,128]{2,1,0:T(2,128)}, f32[24,2,128]{2,1,0:T(2,128)S(1)}, u32[]{:S(2)}, u32[]{:S(2)}) collective-permute-start(f32[24,2,128]{2,1,0:T(2,128)} %get-tuple-element.16.refs_2_), channel_id=1, source_target_pairs={{2,0},{3,1},{0,2},{1,3},{6,4},{7,5},{4,6},{5,7},{10,8},{11,9},{8,1... | collective-permute-start | bytes 73736 | tf_op jit(solution)/shard_map/ppermute | solution.py:298
  9.4 7.5 %pack.1 = (f32[4,40,2,128]{3,2,1,0:T(2,128)}, f32[4,40,2,128]{3,2,1,0:T(2,128)}, f32[4,2,24,128]{3,2,1,0:T(8,128)}) custom-call(f32[4,40,24,128]{3,2,1,0:T(8,128)} %state_ref.3), custom_call_target="tpu_custom_call" | custom-call | flops 49152000 | bytes 2457600 | tf_op jit(solution)/shard_map/pack/pallas_call | solution.py:330
  16.9 3.4 %collective-permute-start.10 = (f32[4,40,2,128]{3,2,1,0:T(2,128)}, f32[4,40,2,128]{3,2,1,0:T(2,128)S(1)}, u32[]{:S(2)}, u32[]{:S(2)}) collective-permute-start(f32[4,40,2,128]{3,2,1,0:T(2,128)} %get-tuple-element.24), channel_id=1, source_target_pairs={{3,0},{0,1},{1,2},{2,3},{7,4},{4,5},{5,6},{6,7},{11,8},{8,9},{9,10... | collective-permute-start | bytes 491528 | tf_op jit(solution)/shard_map/ppermute | solution.py:298
  20.3 0.4 collective-permute-start.11
  20.7 0.0 collective-permute-done.1.refs_4_
  20.8 0.0 collective-permute-done.2.refs_5_
  20.8 0.6 %copy-done.11 = f32[24,2,128]{2,1,0:T(2,128)} copy-done((f32[24,2,128]{2,1,0:T(2,128)}, f32[24,2,128]{2,1,0:T(2,128)S(1)}, u32[]{:S(2)}) %copy-start.11) | copy-done | bytes 24600
  21.4 0.0 copy-done.9
  21.4 0.0 copy-done.10
  21.4 1.7 %middle.1 = (f32[32,128]{1,0:T(8,128)}, f32[320,128]{1,0:T(8,128)}, f32[320,128]{1,0:T(8,128)}, f32[192,128]{1,0:T(8,128)}) custom-call(s32[1]{0:T(128)} %bitcast.refs_0_, f32[4,2,24,128]{3,2,1,0:T(8,128)} %get-tuple-element.15.refs_1_, f32[24,2,128]{2,1,0:T(2,128)} %get-tuple-element.16.refs_2_, f32[26,2,128]{2,1,0:T(2,128)} %copy-done.9, ...), custom_call_target="tpu_custom_call" | custom-call | tf_op jit(solution)/shard_map/middle/pallas_call | solution.py:350
  23.1 0.5 collective-permute-start.3
  23.6 0.0 collective-permute-start.9
  23.6 1.5 %collective-permute-start.8 = (f32[192,128]{1,0:T(8,128)}, f32[192,128]{1,0:T(8,128)S(1)}, u32[]{:S(2)}, u32[]{:S(2)}) collective-permute-start(f32[192,128]{1,0:T(8,128)} %get-tuple-element.19.refs_1_), channel_id=1, source_target_pairs={{24,0},{28,4},{0,8},{4,12},{8,16},{12,20},{16,24},{20,28},{25,1},{... | collective-permute-start | bytes 294920 | tf_op jit(solution)/shard_map/ppermute | solution.py:298
  25.1 0.7 %collective-permute-done.10.below_ref = f32[4,40,2,128]{3,2,1,0:T(2,128)S(1)} collective-permute-done((f32[4,40,2,128]{3,2,1,0:T(2,128)}, f32[4,40,2,128]{3,2,1,0:T(2,128)S(1)}, u32[]{:S(2)}, u32[]{:S(2)}) %collective-permute-start.10) | collective-permute-done | bytes 163872 | tf_op jit(solution)/shard_map/ppermute | solution.py:298
  25.8 1.3 %collective-permute-start.7 = (f32[192,128]{1,0:T(8,128)}, f32[192,128]{1,0:T(8,128)S(1)}, u32[]{:S(2)}, u32[]{:S(2)}) collective-permute-start(f32[192,128]{1,0:T(8,128)} %get-tuple-element.19.refs_1_), channel_id=1, source_target_pairs={{20,0},{24,4},{28,8},{0,12},{4,16},{8,20},{12,24},{16,28},{21,1},{... | collective-permute-start | bytes 294920 | tf_op jit(solution)/shard_map/ppermute | solution.py:298
  27.1 0.5 %collective-permute-done.11.above_ref = f32[4,40,2,128]{3,2,1,0:T(2,128)S(1)} collective-permute-done((f32[4,40,2,128]{3,2,1,0:T(2,128)}, f32[4,40,2,128]{3,2,1,0:T(2,128)S(1)}, u32[]{:S(2)}, u32[]{:S(2)}) %collective-permute-start.11) | collective-permute-done | bytes 163872 | tf_op jit(solution)/shard_map/ppermute | solution.py:298
  27.6 1.5 %collective-permute-start.6 = (f32[192,128]{1,0:T(8,128)}, f32[192,128]{1,0:T(8,128)S(1)}, u32[]{:S(2)}, u32[]{:S(2)}) collective-permute-start(f32[192,128]{1,0:T(8,128)} %get-tuple-element.19.refs_1_), channel_id=1, source_target_pairs={{16,0},{20,4},{24,8},{28,12},{0,16},{4,20},{8,24},{12,28},{17,1},{... | collective-permute-start | bytes 294920 | tf_op jit(solution)/shard_map/ppermute | solution.py:298
  29.1 1.7 %collective-permute-start.5 = (f32[192,128]{1,0:T(8,128)}, f32[192,128]{1,0:T(8,128)S(1)}, u32[]{:S(2)}, u32[]{:S(2)}) collective-permute-start(f32[192,128]{1,0:T(8,128)} %get-tuple-element.19.refs_1_), channel_id=1, source_target_pairs={{12,0},{16,4},{20,8},{24,12},{28,16},{0,20},{4,24},{8,28},{13,1},{... | collective-permute-start | bytes 294920 | tf_op jit(solution)/shard_map/ppermute | solution.py:298
  30.7 0.6 %collective-permute-done.9.refs_8_.got_w_ref = f32[320,128]{1,0:T(8,128)S(1)} collective-permute-done((f32[320,128]{1,0:T(8,128)}, f32[320,128]{1,0:T(8,128)S(1)}, u32[]{:S(2)}, u32[]{:S(2)}) %collective-permute-start.9) | collective-permute-done | bytes 163872 | tf_op jit(solution)/shard_map/ppermute | solution.py:298
  31.3 1.0 %collective-permute-start.4 = (f32[192,128]{1,0:T(8,128)}, f32[192,128]{1,0:T(8,128)S(1)}, u32[]{:S(2)}, u32[]{:S(2)}) collective-permute-start(f32[192,128]{1,0:T(8,128)} %get-tuple-element.19.refs_1_), channel_id=1, source_target_pairs={{8,0},{12,4},{16,8},{20,12},{24,16},{28,20},{0,24},{4,28},{9,1},{1... | collective-permute-start | bytes 294920 | tf_op jit(solution)/shard_map/ppermute | solution.py:298
  32.3 10.2 %tendency.1 = f32[4,40,24,128]{3,2,1,0:T(8,128)} custom-call(f32[4,40,24,128]{3,2,1,0:T(8,128)} %state_ref.3, f32[4,40,2,128]{3,2,1,0:T(2,128)} %copy-done.2, f32[4,40,2,128]{3,2,1,0:T(2,128)} %copy-done.3, f32[32,128]{1,0:T(8,128)} %get-tuple-element.26.wide_ref, f32[320,128]{1,0:T(8,128)} %get-tuple-element.20.own_w_ref, ...), custom_call_target="tpu_custom_call" | custom-call | flops 49152000 | bytes 4423680 | tf_op jit(solution)/shard_map/tendency/pallas_call | solution.py:366
  42.5 0.0 collective-permute-done.7.refs_6_
  42.5 0.0 collective-permute-done.6.refs_5_
  42.6 0.6 %copy-done.4 = f32[192,128]{1,0:T(8,128)} copy-done((f32[192,128]{1,0:T(8,128)}, f32[192,128]{1,0:T(8,128)S(1)}, u32[]{:S(2)}) %copy-start.4) | copy-done | bytes 98328
  43.1 0.0 copy-done.5
  43.2 0.1 copy-done.6
  43.2 0.0 copy-done.7
  43.3 0.6 %copy-done.8 = f32[192,128]{1,0:T(8,128)} copy-done((f32[192,128]{1,0:T(8,128)}, f32[192,128]{1,0:T(8,128)S(1)}, u32[]{:S(2)}) %copy-start.8) | copy-done | bytes 98328
  43.9 5.0 %solve.1 = (f32[24,128]{1,0:T(8,128)}, f32[24,128]{1,0:T(8,128)}) custom-call(s32[1]{0:T(128)} %bitcast.refs_0_, f32[192,128]{1,0:T(8,128)} %get-tuple-element.19.refs_1_, f32[320,128]{1,0:T(8,128)} %copy-done, f32[192,128]{1,0:T(8,128)} %copy-done.8, f32[192,128]{1,0:T(8,128)} %copy-done.7, f32[192,128]{1,0:T(8,128)} %copy-done.6, f32[192,128]{1,0:T(8,128)} %copy-done.5, ...), custom_call_target="tpu_custom_call" | custom-call | tf_op jit(solution)/shard_map/solve/pallas_call | solution.py:384
  (21 shorter events, 0.0 us)
Async XLA Ops:
  3.3 17.4 %collective-permute-start = (f32[26,2,128]{2,1,0:T(2,128)}, f32[26,2,128]{2,1,0:T(2,128)S(1)}, u32[]{:S(2)}, u32[]{:S(2)}) collective-permute-start(f32[26,2,128]{2,1,0:T(2,128)} %get-tuple-element.17), channel_id=1, source_target_pairs={{1,0},{2,1},{3,2},{0,3},{5,4},{6,5},{7,6},{4,7},{9,8},{10,9},{11,1... | collective-permute-start | bytes 79880 | tf_op jit(solution)/shard_map/ppermute | solution.py:298
  8.4 12.4 %collective-permute-start.2 = (f32[26,2,128]{2,1,0:T(2,128)}, f32[26,2,128]{2,1,0:T(2,128)S(1)}, u32[]{:S(2)}, u32[]{:S(2)}) collective-permute-start(f32[26,2,128]{2,1,0:T(2,128)} %get-tuple-element.18), channel_id=1, source_target_pairs={{3,0},{0,1},{1,2},{2,3},{7,4},{4,5},{5,6},{6,7},{11,8},{8,9},{9,10... | collective-permute-start | bytes 79880 | tf_op jit(solution)/shard_map/ppermute | solution.py:298
  8.4 12.3 %collective-permute-start.1 = (f32[24,2,128]{2,1,0:T(2,128)}, f32[24,2,128]{2,1,0:T(2,128)S(1)}, u32[]{:S(2)}, u32[]{:S(2)}) collective-permute-start(f32[24,2,128]{2,1,0:T(2,128)} %get-tuple-element.16.refs_2_), channel_id=1, source_target_pairs={{2,0},{3,1},{0,2},{1,3},{6,4},{7,5},{4,6},{5,7},{10,8},{11,9},{8,1... | collective-permute-start | bytes 73736 | tf_op jit(solution)/shard_map/ppermute | solution.py:298
  16.9 8.9 %collective-permute-start.10 = (f32[4,40,2,128]{3,2,1,0:T(2,128)}, f32[4,40,2,128]{3,2,1,0:T(2,128)S(1)}, u32[]{:S(2)}, u32[]{:S(2)}) collective-permute-start(f32[4,40,2,128]{3,2,1,0:T(2,128)} %get-tuple-element.24), channel_id=1, source_target_pairs={{3,0},{0,1},{1,2},{2,3},{7,4},{4,5},{5,6},{6,7},{11,8},{8,9},{9,10... | collective-permute-start | bytes 491528 | tf_op jit(solution)/shard_map/ppermute | solution.py:298
  20.3 7.3 %collective-permute-start.11 = (f32[4,40,2,128]{3,2,1,0:T(2,128)}, f32[4,40,2,128]{3,2,1,0:T(2,128)S(1)}, u32[]{:S(2)}, u32[]{:S(2)}) collective-permute-start(f32[4,40,2,128]{3,2,1,0:T(2,128)} %get-tuple-element.25), channel_id=1, source_target_pairs={{1,0},{2,1},{3,2},{0,3},{5,4},{6,5},{7,6},{4,7},{9,8},{10,9},{11,1... | collective-permute-start | bytes 491528 | tf_op jit(solution)/shard_map/ppermute | solution.py:298
  20.7 0.6 %copy-start.11 = (f32[24,2,128]{2,1,0:T(2,128)}, f32[24,2,128]{2,1,0:T(2,128)S(1)}, u32[]{:S(2)}) copy-start(f32[24,2,128]{2,1,0:T(2,128)S(1)} %collective-permute-done.1.refs_4_) | copy-start | bytes 73732
  20.8 0.6 %copy-start.9 = (f32[26,2,128]{2,1,0:T(2,128)}, f32[26,2,128]{2,1,0:T(2,128)S(1)}, u32[]{:S(2)}) copy-start(f32[26,2,128]{2,1,0:T(2,128)S(1)} %collective-permute-done.refs_3_) | copy-start | bytes 79876
  20.8 0.6 %copy-start.10 = (f32[26,2,128]{2,1,0:T(2,128)}, f32[26,2,128]{2,1,0:T(2,128)S(1)}, u32[]{:S(2)}) copy-start(f32[26,2,128]{2,1,0:T(2,128)S(1)} %collective-permute-done.2.refs_5_) | copy-start | bytes 79876
  23.1 6.0 %collective-permute-start.3 = (f32[320,128]{1,0:T(8,128)}, f32[320,128]{1,0:T(8,128)S(1)}, u32[]{:S(2)}, u32[]{:S(2)}) collective-permute-start(f32[320,128]{1,0:T(8,128)} %get-tuple-element.20.own_w_ref), channel_id=1, source_target_pairs={{4,0},{8,4},{12,8},{16,12},{20,16},{24,20},{28,24},{0,28},{5,1},{9... | collective-permute-start | bytes 491528 | tf_op jit(solution)/shard_map/ppermute | solution.py:298
  23.6 7.7 %collective-permute-start.9 = (f32[320,128]{1,0:T(8,128)}, f32[320,128]{1,0:T(8,128)S(1)}, u32[]{:S(2)}, u32[]{:S(2)}) collective-permute-start(f32[320,128]{1,0:T(8,128)} %get-tuple-element.21.own_e_ref), channel_id=1, source_target_pairs={{28,0},{0,4},{4,8},{8,12},{12,16},{16,20},{20,24},{24,28},{29,1},{... | collective-permute-start | bytes 491528 | tf_op jit(solution)/shard_map/ppermute | solution.py:298
  23.6 18.8 %collective-permute-start.8 = (f32[192,128]{1,0:T(8,128)}, f32[192,128]{1,0:T(8,128)S(1)}, u32[]{:S(2)}, u32[]{:S(2)}) collective-permute-start(f32[192,128]{1,0:T(8,128)} %get-tuple-element.19.refs_1_), channel_id=1, source_target_pairs={{24,0},{28,4},{0,8},{4,12},{8,16},{12,20},{16,24},{20,28},{25,1},{... | collective-permute-start | bytes 294920 | tf_op jit(solution)/shard_map/ppermute | solution.py:298
  25.8 6.5 %copy-start.2 = (f32[4,40,2,128]{3,2,1,0:T(2,128)}, f32[4,40,2,128]{3,2,1,0:T(2,128)S(1)}, u32[]{:S(2)}) copy-start(f32[4,40,2,128]{3,2,1,0:T(2,128)S(1)} %collective-permute-done.10.below_ref) | copy-start | bytes 491524
  25.8 16.7 %collective-permute-start.7 = (f32[192,128]{1,0:T(8,128)}, f32[192,128]{1,0:T(8,128)S(1)}, u32[]{:S(2)}, u32[]{:S(2)}) collective-permute-start(f32[192,128]{1,0:T(8,128)} %get-tuple-element.19.refs_1_), channel_id=1, source_target_pairs={{20,0},{24,4},{28,8},{0,12},{4,16},{8,20},{12,24},{16,28},{21,1},{... | collective-permute-start | bytes 294920 | tf_op jit(solution)/shard_map/ppermute | solution.py:298
  27.6 4.7 %copy-start.3 = (f32[4,40,2,128]{3,2,1,0:T(2,128)}, f32[4,40,2,128]{3,2,1,0:T(2,128)S(1)}, u32[]{:S(2)}) copy-start(f32[4,40,2,128]{3,2,1,0:T(2,128)S(1)} %collective-permute-done.11.above_ref) | copy-start | bytes 491524
  27.6 15.0 %collective-permute-start.6 = (f32[192,128]{1,0:T(8,128)}, f32[192,128]{1,0:T(8,128)S(1)}, u32[]{:S(2)}, u32[]{:S(2)}) collective-permute-start(f32[192,128]{1,0:T(8,128)} %get-tuple-element.19.refs_1_), channel_id=1, source_target_pairs={{16,0},{20,4},{24,8},{28,12},{0,16},{4,20},{8,24},{12,28},{17,1},{... | collective-permute-start | bytes 294920 | tf_op jit(solution)/shard_map/ppermute | solution.py:298
  29.1 3.2 %copy-start = (f32[320,128]{1,0:T(8,128)}, f32[320,128]{1,0:T(8,128)S(1)}, u32[]{:S(2)}) copy-start(f32[320,128]{1,0:T(8,128)S(1)} %collective-permute-done.3.refs_2_.got_e_ref) | copy-start | bytes 491524
  29.1 13.5 %collective-permute-start.5 = (f32[192,128]{1,0:T(8,128)}, f32[192,128]{1,0:T(8,128)S(1)}, u32[]{:S(2)}, u32[]{:S(2)}) collective-permute-start(f32[192,128]{1,0:T(8,128)} %get-tuple-element.19.refs_1_), channel_id=1, source_target_pairs={{12,0},{16,4},{20,8},{24,12},{28,16},{0,20},{4,24},{8,28},{13,1},{... | collective-permute-start | bytes 294920 | tf_op jit(solution)/shard_map/ppermute | solution.py:298
  31.3 1.0 %copy-start.1 = (f32[320,128]{1,0:T(8,128)}, f32[320,128]{1,0:T(8,128)S(1)}, u32[]{:S(2)}) copy-start(f32[320,128]{1,0:T(8,128)S(1)} %collective-permute-done.9.refs_8_.got_w_ref) | copy-start | bytes 491524
  31.3 11.2 %collective-permute-start.4 = (f32[192,128]{1,0:T(8,128)}, f32[192,128]{1,0:T(8,128)S(1)}, u32[]{:S(2)}, u32[]{:S(2)}) collective-permute-start(f32[192,128]{1,0:T(8,128)} %get-tuple-element.19.refs_1_), channel_id=1, source_target_pairs={{8,0},{12,4},{16,8},{20,12},{24,16},{28,20},{0,24},{4,28},{9,1},{1... | collective-permute-start | bytes 294920 | tf_op jit(solution)/shard_map/ppermute | solution.py:298
  42.5 0.6 %copy-start.4 = (f32[192,128]{1,0:T(8,128)}, f32[192,128]{1,0:T(8,128)S(1)}, u32[]{:S(2)}) copy-start(f32[192,128]{1,0:T(8,128)S(1)} %collective-permute-done.8.refs_7_) | copy-start | bytes 294916
  42.5 0.7 %copy-start.5 = (f32[192,128]{1,0:T(8,128)}, f32[192,128]{1,0:T(8,128)S(1)}, u32[]{:S(2)}) copy-start(f32[192,128]{1,0:T(8,128)S(1)} %collective-permute-done.7.refs_6_) | copy-start | bytes 294916
  42.5 0.7 %copy-start.6 = (f32[192,128]{1,0:T(8,128)}, f32[192,128]{1,0:T(8,128)S(1)}, u32[]{:S(2)}) copy-start(f32[192,128]{1,0:T(8,128)S(1)} %collective-permute-done.6.refs_5_) | copy-start | bytes 294916
  42.5 0.7 %copy-start.7 = (f32[192,128]{1,0:T(8,128)}, f32[192,128]{1,0:T(8,128)S(1)}, u32[]{:S(2)}) copy-start(f32[192,128]{1,0:T(8,128)S(1)} %collective-permute-done.5.refs_4_) | copy-start | bytes 294916
  43.3 0.6 %copy-start.8 = (f32[192,128]{1,0:T(8,128)}, f32[192,128]{1,0:T(8,128)S(1)}, u32[]{:S(2)}) copy-start(f32[192,128]{1,0:T(8,128)S(1)} %collective-permute-done.4.refs_3_) | copy-start | bytes 294916
